TPU v7x, 512 devices: a whole 4x4x16 slice. The times are simulated.
512 devices in a mesh: tm: 4 (over z_hi), mem: 4 (over y), tile: 32 (over x, z_lo, core).
Axes of the slice: x: 4, y: 4, z: 16 (z_hi: 4, z_lo: 4; z = z_hi * 4 + z_lo), core: 2. Of those that a mesh axis runs over, the one named last changes fastest.
Arguments:
- control: float32 [40, 2, 128, 256], P('mem', None, 'tile'), may hold values from -6 to 6
- vertical_modes: float32 [64, 2], replicated, may hold values from -4 to 4
- mode_counts: int32 [128], P('tile'), may hold values from 1 to 2, as said below
- perturbations: bfloat16 [40, 8, 64, 128, 256], P('mem', 'tm', None, 'tile'), may hold values from -6 to 6
- slot_index: int32 [12], P('tm'), may hold values from 0 to 7, as said below
- blend_weight: float32 [12], P('tm'), may hold values from 0 to 1
Outputs:
- increment: float32 [12, 64, 128, 256], P('tm', None, 'tile')
Inputs may be any that keep to these rules, and one draw needn't show every extreme that they name: slot_index[w] // 2 == w // 3. `mode_counts`: both ends of the range occur.
All inputs are finite; a program needn't handle non-finite values.
Results may differ from a plain program's by a relative error of at most 0.0003.
Values sent between devices are 32-bit elements; how exact they have to be, the bound alone decides.
A program may use at most 64 MiB of HBM per device.

v0:
```python
import math

import jax
import jax.numpy as jnp
from jax import lax
from jax.sharding import PartitionSpec as P

VM = 2
SMOOTH = 4


diffusion = 0.24


def padded_2(cells, sides, width):
    for axis, dim in sides:
        count = lax.axis_size(axis)
        head = lax.slice_in_dim(cells, 0, width, axis=dim)
        tail = lax.slice_in_dim(cells, cells.shape[dim] - width, cells.shape[dim], axis=dim)
        cells = jnp.concatenate(
            [
                lax.ppermute(tail, axis, [(i, (i + 1) % count) for i in range(count)]),
                cells,
                lax.ppermute(head, axis, [((i + 1) % count, i) for i in range(count)]),
            ],
            axis=dim,
        )
    return cells


def split_up(x, dim, peers):
    before, after = (x.shape[:dim], x.shape[dim + 1 :])
    return jnp.moveaxis(x.reshape(*before, peers, -1, *after), dim, 0)


def summed_on_arrival(x, axis, dim):
    tiles = split_up(x, dim, lax.axis_size(axis))
    arrived = lax.all_to_all(tiles, axis, split_axis=0, concat_axis=0, tiled=True)
    return arrived.sum(axis=0)


def from_everyone(x, axis):
    copies = jnp.broadcast_to(x, (lax.axis_size(axis), *x.shape))
    return lax.all_to_all(copies, axis, split_axis=0, concat_axis=0, tiled=True)


def joined_by_halves(pieces, combine):
    while len(jax.tree.leaves(pieces)[0]) > 1:
        pieces = jax.vmap(combine)(*(pieces[side::2] for side in (0, 1)))
    return pieces[0]


def prefix(x, axis, combine, identity):
    peers, here = (lax.axis_size(axis), lax.axis_index(axis))
    passed = jnp.arange(peers) < here

    def kept(part, zero, own):
        part = jnp.where(
            passed.reshape(-1, *(1 for _ in own.shape)), part, jnp.asarray(zero, own.dtype)
        )
        return part

    pieces = from_everyone(x, axis)
    return joined_by_halves(kept(pieces, identity, x), combine)


def in_order(tiles, dim):
    tiles = jnp.moveaxis(tiles, 0, dim)
    shape = tiles.shape
    return tiles.reshape(*shape[:dim], shape[dim] * shape[dim + 1], *shape[dim + 2 :])


def gather_directly(x, axis, dim):
    return in_order(from_everyone(x, axis), dim)


def relax_local(padded):
    center = padded[:, :, 1:-1]
    neighbours = padded[:, :, 2:] + padded[:, :, :-2]
    bordered = jnp.pad(center, ((0, 0), (0, 0), (0, 0), (1, 1)))
    lateral = bordered[:, :, :, 2:] + bordered[:, :, :, :-2]
    return center + diffusion * (neighbours + lateral - 4.0 * center)


def add_terms(earlier, later):
    return earlier + later


def per_device(control, vertical_modes, mode_counts, perturbations, slot_index, blend_weight):
    field = padded_2(control, (("tile", 2),), SMOOTH)
    for repeat in range(SMOOTH):
        field = relax_local(field)
    members = perturbations.shape[0]
    slot_count = perturbations.shape[1]
    levels = perturbations.shape[2]
    localized = jnp.zeros((members, levels) + field.shape[2:], jnp.float32)
    for mode_index in range(VM):
        keep_mode = (mode_index < mode_counts).astype(jnp.float32)
        masked = keep_mode[None, :, None] * field[:, mode_index]
        localized = localized + vertical_modes[:, mode_index][None, :, None, None] * masked[:, None]
    partial_sum = jnp.sum(localized[:, None] * perturbations.astype(jnp.float32), axis=0)
    norm_factor = 1.0 / math.sqrt(members * lax.axis_size("mem") - 1)
    member_total = summed_on_arrival(partial_sum, "mem", 1)
    running = jnp.cumsum(member_total * norm_factor, axis=0)
    earlier = prefix(running[-1], "tm", add_terms, jnp.zeros_like(running[-1]))
    extended = jnp.concatenate([earlier[None], earlier[None] + running], axis=0)
    local_slot = slot_index - lax.axis_index("tm") * slot_count
    positions = jnp.arange(slot_count + 1, dtype=jnp.int32)[None, :]
    weight = blend_weight[:, None]
    table = weight * (positions == local_slot[:, None] + 1).astype(jnp.float32)
    table = table + (1.0 - weight) * (positions == local_slot[:, None]).astype(jnp.float32)
    blended = jnp.einsum("we,elxy->wlxy", table, extended, precision=lax.Precision.HIGHEST)
    blended = gather_directly(blended, "mem", 1)
    return blended


def solution(mesh):
    placed = (
        P("mem", None, "tile", None),
        P(),
        P("tile"),
        P("mem", "tm", None, "tile", None),
        P("tm"),
        P("tm"),
    )
    return jax.shard_map(
        per_device,
        mesh=mesh,
        in_specs=placed,
        out_specs=P("tm", None, "tile", None),
        check_vma=False,
    )
```

profile of v0, /device:TPU:36, one launch (start us, length us, event | category | flops | bytes accessed | tf_op | source)
XLA Modules:
  0.0 81.9 jit_solution(17535655725482608220)
XLA Ops:
  0.0 1.9 %collective-permute-start = (f32[10,2,4,256]{3,2,1,0:T(4,128)}, f32[10,2,4,256]{3,2,1,0:T(4,128)S(1)}, u32[]{:S(2)}, u32[]{:S(2)}) collective-permute-start(f32[10,2,4,256]{3,2,1,0:T(4,128)} %param.6), channel_id=1, source_target_pairs={{0,1},{1,2},{2,3},{3,4},{4,5},{5,6},{6,7},{7,8},{8,9},{9,10},{10,1... | collective-permute-start | bytes 245768 | tf_op jit(solution)/shard_map/ppermute | solution.py:22
  1.9 3.6 %collective-permute-start.1 = (f32[10,2,4,256]{3,2,1,0:T(4,128)}, f32[10,2,4,256]{3,2,1,0:T(4,128)S(1)}, u32[]{:S(2)}, u32[]{:S(2)}) collective-permute-start(f32[10,2,4,256]{3,2,1,0:T(4,128)} %param.6), channel_id=1, source_target_pairs={{1,0},{2,1},{3,2},{4,3},{5,4},{6,5},{7,6},{8,7},{9,8},{10,9},{11,1... | collective-permute-start | bytes 245768 | tf_op jit(solution)/shard_map/ppermute | solution.py:24
  5.6 0.8 slice_bitcast_fusion.1
  6.3 0.7 compare_convert_fusion.1
  7.0 0.9 %collective-permute-done.1 = f32[10,2,4,256]{3,2,1,0:T(4,128)S(1)} collective-permute-done((f32[10,2,4,256]{3,2,1,0:T(4,128)}, f32[10,2,4,256]{3,2,1,0:T(4,128)S(1)}, u32[]{:S(2)}, u32[]{:S(2)}) %collective-permute-start.1) | collective-permute-done | bytes 81952 | tf_op jit(solution)/shard_map/ppermute | solution.py:24
  7.9 0.9 %pad_maximum_fusion = f32[10,2,12,256]{3,2,1,0:T(8,128)S(1)} fusion(f32[10,2,4,256]{3,2,1,0:T(4,128)S(1)} %collective-permute-done.1, f32[10,2,4,256]{3,2,1,0:T(4,128)} %param.6, f32[10,2,4,256]{3,2,1,0:T(4,128)S(1)} %collective-permute-done), kind=kLoop, calls=%fused_computation.10 | loop fusion | flops 122880 | bytes 491520 | tf_op jit(solution)/shard_map/concatenate | solution.py:20
  8.9 0.2 fusion.4
  9.2 0.2 fusion.13
  9.4 0.2 fusion.18
  9.8 0.8 multiply_add_fusion
  10.6 0.3 copy-done
  10.9 1.5 %multiply_reduce_fusion = f32[2,64,4,256]{3,2,1,0:T(4,128)S(1)} fusion(bf16[10,2,64,4,256]{4,3,2,1,0:T(4,128)(2,1)S(1)} %copy-done, f32[10,64,4,256]{3,2,1,0:T(4,128)S(1)} %multiply_add_fusion), kind=kLoop, calls=%fused_computation | loop fusion | flops 3801088 | bytes 5767168 | tf_op jit(solution)/shard_map/reduce_sum | solution.py:101
  12.6 0.3 copy.16
  12.9 14.4 %all_to_all.15 = f32[4,2,16,4,256]{4,3,2,1,0:T(4,128)S(1)} all-to-all(f32[4,2,16,4,256]{4,3,2,1,0:T(4,128)S(1)} %copy.16), channel_id=1, replica_groups=mesh['tm'=4,'mem'=4,'tile'=32] {'mem'}, dimensions={0} | all-to-all | bytes 1048576 | tf_op jit(solution)/shard_map/all_to_all | solution.py:38
  27.6 0.3 reduce_window_sum.11
  28.0 0.7 broadcast_in_dim.17
  28.7 14.8 %all-to-all-start.1 = ((f32[4,16,4,256]{3,2,1,0:T(4,128)}), f32[4,16,4,256]{3,2,1,0:T(4,128)S(1)}, u32[]{:S(2)}, u32[]{:S(2)}) async-start(f32[4,16,4,256]{3,2,1,0:T(4,128)} %broadcast_in_dim.17), calls=%async_computation.1 | async-start | bytes 524288 | tf_op jit(solution)/shard_map/all_to_all | solution.py:44
  43.5 19.4 %all-to-all-done.1 = f32[4,16,4,256]{3,2,1,0:T(4,128)S(1)} async-done(((f32[4,16,4,256]{3,2,1,0:T(4,128)}), f32[4,16,4,256]{3,2,1,0:T(4,128)S(1)}, u32[]{:S(2)}, u32[]{:S(2)}) %all-to-all-start.1) | async-done | bytes 262176 | tf_op jit(solution)/shard_map/all_to_all | solution.py:44
  62.9 0.2 copy_select_fusion
  63.1 0.5 slice.114
  63.6 0.5 slice.115
  64.3 0.6 fusion.5
  65.2 15.1 %all_to_all.16 = f32[4,3,16,4,256]{4,3,2,1,0:T(4,128)S(1)} all-to-all(f32[4,3,16,4,256]{4,3,2,1,0:T(4,128)S(1)} %broadcast_in_dim.19), channel_id=1, replica_groups=mesh['tm'=4,'mem'=4,'tile'=32] {'mem'}, dimensions={0} | all-to-all | bytes 1572864 | tf_op jit(solution)/shard_map/all_to_all | solution.py:44
  80.5 1.4 %copy.21 = f32[3,64,4,256]{3,2,1,0:T(4,128)} copy(f32[3,64,4,256]{3,1,2,0:T(8,128)S(1)} %bitcast.25) | data formatting | bytes 1572864 | tf_op jit(solution)/shard_map/reshape | solution.py:70
  (27 shorter events, 1.4 us)
Async XLA Ops:
  0.0 7.0 %collective-permute-start = (f32[10,2,4,256]{3,2,1,0:T(4,128)}, f32[10,2,4,256]{3,2,1,0:T(4,128)S(1)}, u32[]{:S(2)}, u32[]{:S(2)}) collective-permute-start(f32[10,2,4,256]{3,2,1,0:T(4,128)} %param.6), channel_id=1, source_target_pairs={{0,1},{1,2},{2,3},{3,4},{4,5},{5,6},{6,7},{7,8},{8,9},{9,10},{10,1... | collective-permute-start | bytes 245768 | tf_op jit(solution)/shard_map/ppermute | solution.py:22
  1.9 6.0 %collective-permute-start.1 = (f32[10,2,4,256]{3,2,1,0:T(4,128)}, f32[10,2,4,256]{3,2,1,0:T(4,128)S(1)}, u32[]{:S(2)}, u32[]{:S(2)}) collective-permute-start(f32[10,2,4,256]{3,2,1,0:T(4,128)} %param.6), channel_id=1, source_target_pairs={{1,0},{2,1},{3,2},{4,3},{5,4},{6,5},{7,6},{8,7},{9,8},{10,9},{11,1... | collective-permute-start | bytes 245768 | tf_op jit(solution)/shard_map/ppermute | solution.py:24
  9.2 1.7 %copy-start = (bf16[10,2,64,4,256]{4,3,2,1,0:T(4,128)(2,1)S(1)}, bf16[10,2,64,4,256]{4,3,2,1,0:T(4,128)(2,1)}, u32[]{:S(2)}) copy-start(bf16[10,2,64,4,256]{4,3,2,1,0:T(4,128)(2,1)} %param.9) | copy-start | bytes 7864324
  12.4 31.0 %copy-start.1 = (f32[3]{0:T(128)S(1)}, f32[3]{0:T(128)}, u32[]{:S(2)}) copy-start(f32[3]{0:T(128)} %param.11) | copy-start | bytes 40
  12.4 31.1 %copy-start.2 = (s32[3]{0:T(128)S(1)}, s32[3]{0:T(128)}, u32[]{:S(2)}) copy-start(s32[3]{0:T(128)} %param.10) | copy-start | bytes 40
  28.7 34.2 %all-to-all-start.1 = ((f32[4,16,4,256]{3,2,1,0:T(4,128)}), f32[4,16,4,256]{3,2,1,0:T(4,128)S(1)}, u32[]{:S(2)}, u32[]{:S(2)}) async-start(f32[4,16,4,256]{3,2,1,0:T(4,128)} %broadcast_in_dim.17), calls=%async_computation.1 | async-start | bytes 524288 | tf_op jit(solution)/shard_map/all_to_all | solution.py:44
where the time goes:
time: 82.3 us; the launch traced here: 81.9 us
  blocking collectives  29.6 us (36%)
  starting transfers between devices  20.3 us (25%)
  waiting for transfers between devices  20.3 us (25%)
  other arithmetic  5.64 us (7%)
  local copies, waits for them, and re-layouts  5.13 us (6%)
    all_to_all x1, waiting for transfers between devices, from_everyone(): return lax.all_to_all(copies, axis, split_axis=0, concat_axis=0, tiled=True)  19.4 us
    all_to_all x1, blocking collectives, from_everyone(): return lax.all_to_all(copies, axis, split_axis=0, concat_axis=0, tiled=True)  15.1 us
    all_to_all x1, starting transfers between devices, from_everyone(): return lax.all_to_all(copies, axis, split_axis=0, concat_axis=0, tiled=True)  14.8 us
    all_to_all x1, blocking collectives, summed_on_arrival(): lax.all_to_all(tiles, axis, split_axis=0, concat_axis=0, tiled=True)  14.4 us
    ppermute x1, starting transfers between devices, padded_2(): lax.ppermute(head, axis, [((i + 1) % count, i) for i in range(count)])  3.64 us
    ppermute x1, starting transfers between devices, padded_2(): lax.ppermute(tail, axis, [(i, (i + 1) % count) for i in range(count)])  1.91 us
  transfers between devices with their start and end apart: 3, of which 2 were waited for; matrix products, arithmetic and copies ran while one was open for 2% of the time, Pallas kernels for 0%

commit v1 on v0

v1 whole, which is shorter than its diff:
```python
import functools
import math

import jax
import jax.numpy as jnp
from jax import lax
from jax.experimental import pallas as pl
from jax.experimental.pallas import tpu as pltpu
from jax.sharding import PartitionSpec as P

SMOOTH = 4
DIFFUSION = 0.24
CHUNKS = 4
MESH = pl.DeviceIdType.MESH


def smooth_group(halo, f_ref, counts, norm, group, rows):
    lane = lax.broadcasted_iota(jnp.int32, (rows, 128), 1)
    first, last = lane == 0, lane == 127
    base = group * 64

    def load(x, h):
        tile, inner = (x + 4) // 4, x % 4
        return halo[tile, pl.ds(base + h * 4 + inner, rows, 8), :]

    field = {(x, h): load(x, h) for x in range(-4, 8) for h in range(2)}
    for step in range(SMOOTH):
        lo, hi = -3 + step, 7 - step
        new = {}
        for x in range(lo, hi):
            pair = [field[x, 0], field[x, 1]]
            up = [pltpu.roll(v, 1, 1) for v in pair]
            down = [pltpu.roll(v, 127, 1) for v in pair]
            lateral = [
                jnp.where(first, 0.0, up[0]) + jnp.where(last, down[1], down[0]),
                jnp.where(first, up[0], up[1]) + jnp.where(last, 0.0, down[1]),
            ]
            for h in range(2):
                near = field[x - 1, h] + field[x + 1, h]
                new[x, h] = (1.0 - 4.0 * DIFFUSION) * pair[h] + DIFFUSION * (
                    near + lateral[h]
                )
        field = new
    mode = lax.broadcasted_iota(jnp.int32, (rows, 128), 0) % 2
    for x in range(4):
        scales = [jnp.where(m < counts[x], norm, 0.0) for m in range(2)]
        scale = jnp.where(mode == 0, scales[0], scales[1])
        for h in range(2):
            f_ref[pl.ds(base + h * 4 + x, rows, 8), :] = field[x, h] * scale


def kernel(
    n_tm, n_mem, n_tile, members, windows,
    ctrl, pert_hbm, modes, counts, slot_index, weight,
    out,
    halo, pert, f_ref, far, near_r, near_l, mail_a, mail_b, mail_r, mail_l,
    za_out, za_in, zb_in, gath,
    load_sems, halo_send, halo_recv, send, recv,
):
    t, m = lax.axis_index("tm"), lax.axis_index("mem")
    tile = lax.axis_index("tile")
    nc = far.shape[0]
    lc = far.shape[2]
    pairs = lc // 2
    quarter_pairs = nc * pairs
    norm = 1.0 / math.sqrt(members * n_mem - 1)

    ctrl_load = pltpu.make_async_copy(ctrl, halo.at[1], load_sems.at[0])
    ctrl_load.start()
    pert_load = pltpu.make_async_copy(pert_hbm, pert, load_sems.at[1])
    pert_load.start()

    tile_r, tile_l = lax.rem(tile + 1, n_tile), lax.rem(tile + n_tile - 1, n_tile)
    mem_r, mem_l = lax.rem(m + 1, n_mem), lax.rem(m + n_mem - 1, n_mem)
    mem_f = lax.rem(m + 2, n_mem)
    tm_r, tm_l = lax.rem(t + 1, n_tm), lax.rem(t + n_tm - 1, n_tm)
    barrier = pltpu.get_barrier_semaphore()
    partners = (
        {"tile": tile_r}, {"tile": tile_l}, {"mem": mem_r}, {"mem": mem_l},
        {"mem": mem_f}, {"tm": tm_r}, {"tm": tm_l},
    )
    for partner in partners:
        pl.semaphore_signal(barrier, inc=1, device_id=partner, device_id_type=MESH)
    ctrl_load.wait()
    pl.semaphore_wait(barrier, len(partners))

    def remote(src, dst, s, r, device):
        return pltpu.make_async_remote_copy(
            src_ref=src, dst_ref=dst, send_sem=s, recv_sem=r,
            device_id=device, device_id_type=MESH,
        )

    to_right = remote(halo.at[1], halo.at[0], halo_send.at[0], halo_recv.at[0], {"tile": tile_r})
    to_left = remote(halo.at[1], halo.at[2], halo_send.at[1], halo_recv.at[1], {"tile": tile_l})
    to_right.start()
    to_left.start()
    to_right.wait()
    to_left.wait()

    fields = 2 * members
    for group in range(0, fields, 8):
        smooth_group(halo, f_ref, counts, norm, group // 8, min(8, fields - group))
    pert_load.wait()

    def part(quarter, chunk, store):
        def body(p, carry):
            lp = quarter * quarter_pairs + chunk * pairs + p
            v = [[modes[mode, 2 * lp + j] for mode in range(2)] for j in range(2)]
            acc = [[None, None], [None, None]]
            for k in range(members):
                f0 = f_ref[pl.ds(16 * k, 8), :]
                f1 = f_ref[pl.ds(16 * k + 8, 8), :]
                loc = [v[j][0] * f0 + v[j][1] * f1 for j in range(2)]
                for s in range(2):
                    x = pert[k, s, lp].astype(jnp.float32)
                    for j in range(2):
                        term = loc[j] * x[8 * j : 8 * j + 8]
                        acc[s][j] = term if k == 0 else acc[s][j] + term
            for s in range(2):
                for j in range(2):
                    store(s, 2 * p + j, acc[s][j])
            return carry

        lax.fori_loop(0, pairs, body, 0)

    def into(ref):
        def store(s, level, value):
            ref[s, level] = value
        return store

    def channel(k, chunk, src, dst, device):
        return remote(src, dst, send.at[k, chunk], recv.at[k, chunk], device)

    right, left = {"mem": mem_r}, {"mem": mem_l}
    across = {"mem": mem_f}
    onward = {"tm": tm_r}
    back = {"tm": tm_l}

    far_r = [channel(0, c, far.at[c, 0], mail_a.at[c], right) for c in range(nc)]
    far_l = [channel(1, c, far.at[c, 1], mail_b.at[c], left) for c in range(nc)]
    sum_r = [channel(2, c, near_r.at[c], mail_r.at[c], right) for c in range(nc)]
    sum_l = [channel(3, c, near_l.at[c], mail_l.at[c], left) for c in range(nc)]
    chain = [channel(4, c, za_out.at[c], za_in.at[c], onward) for c in range(nc)]
    around = [channel(5, c, za_out.at[c], zb_in.at[c], back) for c in range(nc)]
    relay = [channel(5, c, zb_in.at[c], zb_in.at[c], back) for c in range(nc)]
    slots_r = [channel(6, c, gath.at[m, c, pl.ds(0, 2)], gath.at[m, c, pl.ds(0, 2)], right) for c in range(nc)]
    slots_l = [channel(7, c, gath.at[m, c, pl.ds(0, 2)], gath.at[m, c, pl.ds(0, 2)], left) for c in range(nc)]
    pass_r = [channel(8, c, gath.at[mem_l, c, 0], gath.at[mem_l, c, 0], right) for c in range(nc)]
    pass_l = [channel(9, c, gath.at[mem_r, c, 1], gath.at[mem_r, c, 1], left) for c in range(nc)]
    early_r = [channel(10, c, gath.at[m, c, 2], gath.at[m, c, 2], right) for c in range(nc)]
    early_l = [channel(11, c, gath.at[m, c, 2], gath.at[m, c, 2], left) for c in range(nc)]
    early_f = [channel(12, c, gath.at[m, c, 2], gath.at[m, c, 2], across) for c in range(nc)]

    for c in range(nc):
        part(mem_f, c, into(far.at[c]))
        far_r[c].start()
        far_l[c].start()
    for c in range(nc):
        part(mem_r, c, into(near_r.at[c]))
        part(mem_l, c, into(near_l.at[c]))
    for c in range(nc):
        part(m, c, into(gath.at[m, c]))

    for c in range(nc):
        far_r[c].wait_recv()
        near_r[c, 0] += mail_a[c]
        sum_r[c].start()
        far_l[c].wait_recv()
        near_l[c, 1] += mail_b[c]
        sum_l[c].start()

    for c in range(nc):
        sum_r[c].wait_recv()
        sum_l[c].wait_recv()
        total = jnp.zeros_like(za_out[c])
        for s in range(2):
            value = gath[m, c, s] + (mail_r[c, s] + mail_l[c, s])
            gath[m, c, s] = value
            total = total + value
        za_out[c] = total

        @pl.when(t < 2)
        def _():
            chain[c].start()

        @pl.when(t == 0)
        def _():
            around[c].start()

        slots_r[c].start()
        slots_l[c].start()

    for c in range(nc):
        slots_r[c].wait_recv()
        pass_r[c].start()
        slots_l[c].wait_recv()
        pass_l[c].start()

    for c in range(nc):
        @pl.when(t == 2)
        def _():
            chain[c].wait_recv()
            za_out[c] += za_in[c]
            chain[c].start()

        @pl.when(t == 3)
        def _():
            around[c].wait_recv()
            relay[c].start()

    for c in range(nc):
        pass_r[c].wait_recv()
        pass_l[c].wait_recv()

    for c in range(nc):
        @pl.when(t == 0)
        def _():
            gath[m, c, 2] = jnp.zeros_like(gath[m, c, 2])

        @pl.when(t == 1)
        def _():
            chain[c].wait_recv()
            gath[m, c, 2] = za_in[c]

        @pl.when(t == 2)
        def _():
            relay[c].wait_recv()
            gath[m, c, 2] = za_in[c] + zb_in[c]

        @pl.when(t == 3)
        def _():
            chain[c].wait_recv()
            gath[m, c, 2] = za_in[c] + zb_in[c]

        early_r[c].start()
        early_l[c].start()
        early_f[c].start()

    scale = []
    for w in range(windows):
        b = weight[w]
        later = slot_index[w] - 2 * t == 1
        scale.append((jnp.where(later, 1.0, b), jnp.where(later, b, 0.0)))

    for c in range(nc):
        early_r[c].wait_recv()
        early_l[c].wait_recv()
        early_f[c].wait_recv()
        for q in range(n_mem):
            def body(level, carry):
                r0, r1, e = (gath[q, c, i, level] for i in range(3))
                for w in range(windows):
                    out[w, q * nc * lc + c * lc + level] = e + (scale[w][0] * r0 + scale[w][1] * r1)
                return carry
            lax.fori_loop(0, lc, body, 0)

    for group in (far_r, far_l, sum_r, sum_l, slots_r, slots_l, pass_r, pass_l, early_r, early_l, early_f):
        for copy in group:
            copy.wait_send()
    for c in range(nc):
        @pl.when(t < 3)
        def _():
            chain[c].wait_send()

        @pl.when(t == 0)
        def _():
            around[c].wait_send()

        @pl.when(t == 3)
        def _():
            relay[c].wait_send()


def solution(mesh):
    n_tm, n_mem, n_tile = (mesh.shape[a] for a in ("tm", "mem", "tile"))

    def folded(x):
        *lead, rows, columns = x.shape
        x = x.reshape(*lead, rows, columns // 128, 128)
        x = jnp.swapaxes(x, -3, -2)
        return x.reshape(*lead, rows * (columns // 128), 128)

    def per_device(control, vertical_modes, mode_counts, perturbations, slot_index, blend_weight):
        members, slots, levels = perturbations.shape[:3]
        windows = slot_index.shape[0]
        ctrl = folded(control).reshape(-1, 128)
        pert = folded(perturbations).reshape(members, slots, levels // 2, 16, 128)
        rows = ctrl.shape[0]
        nc = CHUNKS
        lc = levels // n_mem // nc
        f32 = jnp.float32
        slot = (nc, slots, lc, 8, 128)
        one = (nc, lc, 8, 128)
        smem = pl.BlockSpec(memory_space=pltpu.SMEM)
        hbm = pl.BlockSpec(memory_space=pl.ANY)
        dma = pltpu.SemaphoreType.DMA
        out = pl.pallas_call(
            functools.partial(kernel, n_tm, n_mem, n_tile, members, windows),
            out_shape=jax.ShapeDtypeStruct((windows, levels, 8, 128), f32),
            in_specs=[hbm, hbm, smem, smem, smem, smem],
            out_specs=pl.BlockSpec(memory_space=pltpu.VMEM),
            scratch_shapes=[
                pltpu.VMEM((3, rows, 128), f32),
                pltpu.VMEM(pert.shape, jnp.bfloat16),
                pltpu.VMEM((rows, 128), f32),
                pltpu.VMEM(slot, f32), pltpu.VMEM(slot, f32), pltpu.VMEM(slot, f32),
                pltpu.VMEM(one, f32), pltpu.VMEM(one, f32),
                pltpu.VMEM(slot, f32), pltpu.VMEM(slot, f32),
                pltpu.VMEM(one, f32), pltpu.VMEM(one, f32), pltpu.VMEM(one, f32),
                pltpu.VMEM((n_mem, nc, 3, lc, 8, 128), f32),
                dma((2,)), dma((2,)), dma((2,)), dma((13, nc)), dma((13, nc)),
            ],
            compiler_params=pltpu.CompilerParams(collective_id=0, has_side_effects=True),
        )(ctrl, pert, vertical_modes.T, mode_counts, slot_index, blend_weight)
        out = out.reshape(windows, levels, 2, 4, 128)
        return jnp.swapaxes(out, -3, -2).reshape(windows, levels, 4, 256)

    return jax.shard_map(
        per_device,
        mesh=mesh,
        in_specs=(
            P("mem", None, "tile", None), P(), P("tile"),
            P("mem", "tm", None, "tile", None), P("tm"), P("tm"),
        ),
        out_specs=P("tm", None, "tile", None),
        check_vma=False,
    )
```

time: 82.3 us -> 43.8 us (0.53)
  the two profiles are of different devices: /device:TPU:36 before, /device:TPU:8 now
where the time goes in v1:
time: 43.8 us; the launch traced here: 43.6 us
  Pallas kernels  41.4 us (95%)
  local copies, waits for them, and re-layouts  2.15 us (5%)
    pallas_call x1, Pallas kernels, per_device(): pl.pallas_call(functools.partial(kernel, n_tm, n_mem, n_tile, members, wi...  41.4 us
    unnamed x1, local copies, waits for them, and re-layouts  2.15 us

profile of v1, /device:TPU:8, one launch (start us, length us, event | category | flops | bytes accessed | tf_op | source)
XLA Modules:
  0.0 43.6 jit_solution(9988249916281697514)
XLA Ops:
  0.0 41.4 %shard_map.64 = f32[3,64,8,128]{3,2,1,0:T(8,128)} custom-call(f32[160,128]{1,0:T(8,128)} %bitcast.18, bf16[10,2,32,16,128]{4,3,2,1,0:T(8,128)(2,1)} %bitcast.17, f32[2,64]{1,0:T(2,128)} %bitcast.19, s32[4]{0:T(128)} %counts.1, s32[3]{0:T(128)} %slot_index.1, f32[3]{0:T(128)} %weight.1), custom_call_target="tpu_custom_call" | custom-call | tf_op jit(solution)/shard_map/pallas_call | solution.py:297
  41.4 2.1 %copy.11 = f32[3,64,4,256]{3,2,1,0:T(4,128)} copy(f32[3,64,4,256]{3,2,1,0:T(4,128)} %bitcast.16) | data formatting | bytes 1572864

commit v2 on v1

v2 whole, which is shorter than its diff:
```python
import functools
import math
from contextlib import nullcontext as scope

import jax
import jax.numpy as jnp
from jax import lax
from jax.experimental import pallas as pl
from jax.experimental.pallas import tpu as pltpu
from jax.sharding import PartitionSpec as P

SMOOTH = 4
DIFFUSION = 0.24
CHUNKS = 4
MESH = pl.DeviceIdType.MESH


def smooth_group(halo, f_ref, counts, norm, group, rows):
    lane = lax.broadcasted_iota(jnp.int32, (rows, 128), 1)
    first, last = lane == 0, lane == 127
    base = group * 64

    def load(x, h):
        tile, inner = (x + 4) // 4, x % 4
        return halo[tile, pl.ds(base + h * 4 + inner, rows, 8), :]

    field = {(x, h): load(x, h) for x in range(-4, 8) for h in range(2)}
    for step in range(SMOOTH):
        lo, hi = -3 + step, 7 - step
        new = {}
        for x in range(lo, hi):
            pair = [field[x, 0], field[x, 1]]
            up = [pltpu.roll(v, 1, 1) for v in pair]
            down = [pltpu.roll(v, 127, 1) for v in pair]
            lateral = [
                jnp.where(first, 0.0, up[0]) + jnp.where(last, down[1], down[0]),
                jnp.where(first, up[0], up[1]) + jnp.where(last, 0.0, down[1]),
            ]
            for h in range(2):
                near = field[x - 1, h] + field[x + 1, h]
                new[x, h] = (1.0 - 4.0 * DIFFUSION) * pair[h] + DIFFUSION * (
                    near + lateral[h]
                )
        field = new
    mode = lax.broadcasted_iota(jnp.int32, (rows, 128), 0) % 2
    for x in range(4):
        scales = [jnp.where(m < counts[x], norm, 0.0) for m in range(2)]
        scale = jnp.where(mode == 0, scales[0], scales[1])
        for h in range(2):
            f_ref[pl.ds(base + h * 4 + x, rows, 8), :] = field[x, h] * scale


def kernel(
    n_tm, n_mem, n_tile, members, windows,
    ctrl, pert_hbm, modes_hbm, counts_hbm, index_hbm, weight_hbm,
    gath, scale,
    halo, pert, f_ref, far, near_r, near_l, mail_a, mail_b, mail_r, mail_l,
    za_out, za_in, zb_in, modes, counts, slot_index, weight,
    load_sems, halo_send, halo_recv, send, recv, ready_next, ready_back,
):
    t, m = lax.axis_index("tm"), lax.axis_index("mem")
    tile = lax.axis_index("tile")
    nc = far.shape[0]
    lc = far.shape[2]
    pairs = lc // 2
    quarter_pairs = nc * pairs
    norm = 1.0 / math.sqrt(members * n_mem - 1)

    tile_r, tile_l = lax.rem(tile + 1, n_tile), lax.rem(tile + n_tile - 1, n_tile)
    mem_r, mem_l = lax.rem(m + 1, n_mem), lax.rem(m + n_mem - 1, n_mem)
    mem_f = lax.rem(m + 2, n_mem)
    tm_r, tm_l = lax.rem(t + 1, n_tm), lax.rem(t + n_tm - 1, n_tm)
    right, left, across = {"mem": mem_r}, {"mem": mem_l}, {"mem": mem_f}
    onward, back = {"tm": tm_r}, {"tm": tm_l}

    def signal(sem, device):
        pl.semaphore_signal(sem, inc=1, device_id=device, device_id_type=MESH)

    barrier = pltpu.get_barrier_semaphore()
    partners = ({"tile": tile_r}, {"tile": tile_l}, right, left, across)
    for partner in partners:
        signal(barrier, partner)

    @pl.when(t < 2)
    def _():
        signal(barrier, onward)

    @pl.when((t == 0) | (t == 3))
    def _():
        signal(barrier, back)

    loads = [
        pltpu.make_async_copy(src, dst, load_sems.at[k])
        for k, (src, dst) in enumerate((
            (ctrl, halo.at[1]), (counts_hbm, counts), (modes_hbm, modes),
            (index_hbm, slot_index), (weight_hbm, weight), (pert_hbm, pert),
        ))
    ]
    for load in loads:
        load.start()
    with scope("barrier"):
        loads[0].wait()
        extra = jnp.where(t == 0, 0, jnp.where(t == 2, 2, 1))
        pl.semaphore_wait(barrier, len(partners) + extra)

    def remote(src, dst, s, r, device):
        return pltpu.make_async_remote_copy(
            src_ref=src, dst_ref=dst, send_sem=s, recv_sem=r,
            device_id=device, device_id_type=MESH,
        )

    to_right = remote(halo.at[1], halo.at[0], halo_send.at[0], halo_recv.at[0], {"tile": tile_r})
    to_left = remote(halo.at[1], halo.at[2], halo_send.at[1], halo_recv.at[1], {"tile": tile_l})
    to_right.start()
    to_left.start()

    @pl.when((t == 1) | (t == 2))
    def _():
        signal(ready_next, back)

    @pl.when(t >= 2)
    def _():
        signal(ready_back, onward)

    for load in loads[1:5]:
        load.wait()
    for w in range(windows):
        b = weight[w]
        later = slot_index[w] - 2 * t == 1
        scale[w, 0] = jnp.full((8, 128), jnp.where(later, 1.0, b), jnp.float32)
        scale[w, 1] = jnp.full((8, 128), jnp.where(later, b, 0.0), jnp.float32)
    with scope("halo"):
        to_right.wait()
        to_left.wait()

    with scope("smooth"):
        fields = 2 * members
        for group in range(0, fields, 8):
            smooth_group(halo, f_ref, counts, norm, group // 8, min(8, fields - group))
        loads[5].wait()

    def part(quarter, chunk, dst):
        def body(p, carry):
            lp = quarter * quarter_pairs + chunk * pairs + p
            v = [[modes[mode, 2 * lp + j] for mode in range(2)] for j in range(2)]
            acc = [[None, None], [None, None]]
            for k in range(members):
                f0 = f_ref[pl.ds(16 * k, 8), :]
                f1 = f_ref[pl.ds(16 * k + 8, 8), :]
                loc = [v[j][0] * f0 + v[j][1] * f1 for j in range(2)]
                for s in range(2):
                    x = pert[k, s, lp].astype(jnp.float32)
                    for j in range(2):
                        term = loc[j] * x[8 * j : 8 * j + 8]
                        acc[s][j] = term if k == 0 else acc[s][j] + term
            for s in range(2):
                for j in range(2):
                    dst[s, 2 * p + j] = acc[s][j]
            return carry

        if pairs == 1:
            body(0, 0)
        else:
            lax.fori_loop(0, pairs, body, 0)

    def channel(k, chunk, src, dst, device):
        return remote(src, dst, send.at[k, chunk], recv.at[k, chunk], device)

    def both(ref):
        return ref.at[pl.ds(0, 2)]

    far_r = [channel(0, c, far.at[c, 0], mail_a.at[c], right) for c in range(nc)]
    far_l = [channel(1, c, far.at[c, 1], mail_b.at[c], left) for c in range(nc)]
    sum_r = [channel(2, c, near_r.at[c], mail_r.at[c], right) for c in range(nc)]
    sum_l = [channel(3, c, near_l.at[c], mail_l.at[c], left) for c in range(nc)]
    chain = [channel(4, c, za_out.at[c], za_in.at[c], onward) for c in range(nc)]
    around = [channel(5, c, za_out.at[c], zb_in.at[c], back) for c in range(nc)]
    relay = [channel(5, c, zb_in.at[c], zb_in.at[c], back) for c in range(nc)]
    slots_r = [channel(6, c, both(gath.at[m, c]), both(gath.at[m, c]), right) for c in range(nc)]
    slots_l = [channel(7, c, both(gath.at[m, c]), both(gath.at[m, c]), left) for c in range(nc)]
    pass_r = [channel(8, c, gath.at[mem_l, c, 0], gath.at[mem_l, c, 0], right) for c in range(nc)]
    pass_l = [channel(9, c, gath.at[mem_r, c, 1], gath.at[mem_r, c, 1], left) for c in range(nc)]
    early_r = [channel(10, c, gath.at[m, c, 2], gath.at[m, c, 2], right) for c in range(nc)]
    early_l = [channel(11, c, gath.at[m, c, 2], gath.at[m, c, 2], left) for c in range(nc)]
    early_f = [channel(12, c, gath.at[m, c, 2], gath.at[m, c, 2], across) for c in range(nc)]

    with scope("far"):
        for c in range(nc):
            part(mem_f, c, far.at[c])
            far_r[c].start()
            far_l[c].start()
    with scope("near"):
        for c in range(nc):
            part(mem_r, c, near_r.at[c])
            part(mem_l, c, near_l.at[c])
        for c in range(nc):
            part(m, c, gath.at[m, c])

    for c in range(nc):
        with scope(f"A{c}"):
            far_r[c].wait_recv()
            near_r[c, 0] += mail_a[c]
            sum_r[c].start()
            far_l[c].wait_recv()
            near_l[c, 1] += mail_b[c]
            sum_l[c].start()

    with scope("R"):
        @pl.when(t < 2)
        def _():
            pl.semaphore_wait(ready_next, 1)

        @pl.when((t == 0) | (t == 3))
        def _():
            pl.semaphore_wait(ready_back, 1)

    for c in range(nc):
        with scope(f"B{c}"):
            sum_r[c].wait_recv()
            sum_l[c].wait_recv()
            for level in range(lc):
                total = None
                for s in range(2):
                    value = gath[m, c, s, level] + (mail_r[c, s, level] + mail_l[c, s, level])
                    gath[m, c, s, level] = value
                    total = value if s == 0 else total + value
                za_out[c, level] = total

            @pl.when(t < 2)
            def _():
                chain[c].start()

            @pl.when(t == 0)
            def _():
                around[c].start()

            slots_r[c].start()
            slots_l[c].start()

    for c in range(nc):
        with scope(f"Z{c}"):
            @pl.when(t == 2)
            def _():
                chain[c].wait_recv()
                za_out[c] += za_in[c]
                chain[c].start()

            @pl.when(t == 3)
            def _():
                around[c].wait_recv()
                relay[c].start()
        with scope(f"D{c}"):
            slots_r[c].wait_recv()
            pass_r[c].start()
            slots_l[c].wait_recv()
            pass_l[c].start()

    for c in range(nc):
        with scope(f"E{c}"):
            @pl.when(t == 0)
            def _():
                gath[m, c, 2] = jnp.zeros_like(gath[m, c, 2])

            @pl.when(t == 1)
            def _():
                chain[c].wait_recv()
                gath[m, c, 2] = za_in[c]

            @pl.when(t == 2)
            def _():
                relay[c].wait_recv()
                gath[m, c, 2] = za_in[c] + zb_in[c]

            @pl.when(t == 3)
            def _():
                chain[c].wait_recv()
                gath[m, c, 2] = za_in[c] + zb_in[c]

            early_r[c].start()
            early_l[c].start()
            early_f[c].start()

    with scope("P"):
        for c in range(nc):
            pass_r[c].wait_recv()
            pass_l[c].wait_recv()

    for c in range(nc):
        with scope(f"H{c}"):
            early_r[c].wait_recv()
            early_l[c].wait_recv()
            early_f[c].wait_recv()

    for group in (far_r, far_l, sum_r, sum_l, slots_r, slots_l, pass_r, pass_l, early_r, early_l, early_f):
        for copy in group:
            copy.wait_send()
    for c in range(nc):
        @pl.when(t < 3)
        def _():
            chain[c].wait_send()

        @pl.when(t == 0)
        def _():
            around[c].wait_send()

        @pl.when(t == 3)
        def _():
            relay[c].wait_send()


def blend_kernel(gath, scale, out, block, sems):
    n_mem, nc, _, lc = gath.shape[:4]
    windows = block.shape[0]
    copies = []
    for w in range(windows):
        a, b = scale[w, 0], scale[w, 1]
        for q in range(n_mem):
            for c in range(nc):
                for level in range(lc):
                    r0, r1, e = (gath[q, c, i, level] for i in range(3))
                    block[w, (q * nc + c) * lc + level] = e + (a * r0 + b * r1)
        copies.append(pltpu.make_async_copy(block.at[w], out.at[w], sems.at[w]))
        copies[-1].start()
    for copy in copies:
        copy.wait()


def solution(mesh):
    n_tm, n_mem, n_tile = (mesh.shape[a] for a in ("tm", "mem", "tile"))

    def folded(x):
        *lead, rows, columns = x.shape
        x = x.reshape(*lead, rows, columns // 128, 128)
        x = jnp.swapaxes(x, -3, -2)
        return x.reshape(*lead, rows * (columns // 128), 128)

    def per_device(control, vertical_modes, mode_counts, perturbations, slot_index, blend_weight):
        members, slots, levels = perturbations.shape[:3]
        windows = slot_index.shape[0]
        ctrl = folded(control).reshape(-1, 128)
        pert = folded(perturbations).reshape(members, slots, levels // 2, 16, 128)
        rows = ctrl.shape[0]
        nc = CHUNKS
        lc = levels // n_mem // nc
        f32 = jnp.float32
        slot = (nc, slots, lc, 8, 128)
        one = (nc, lc, 8, 128)
        vmem = pl.BlockSpec(memory_space=pltpu.VMEM)
        hbm = pl.BlockSpec(memory_space=pl.ANY)
        dma = pltpu.SemaphoreType.DMA
        regular = pltpu.SemaphoreType.REGULAR
        gath, scale = pl.pallas_call(
            functools.partial(kernel, n_tm, n_mem, n_tile, members, windows),
            out_shape=(
                pltpu.VMEM((n_mem, nc, 3, lc, 8, 128), f32),
                pltpu.VMEM((windows, 2, 8, 128), f32),
            ),
            in_specs=[hbm] * 6,
            out_specs=(vmem, vmem),
            scratch_shapes=[
                pltpu.VMEM((3, rows, 128), f32),
                pltpu.VMEM(pert.shape, jnp.bfloat16),
                pltpu.VMEM((rows, 128), f32),
                pltpu.VMEM(slot, f32), pltpu.VMEM(slot, f32), pltpu.VMEM(slot, f32),
                pltpu.VMEM(one, f32), pltpu.VMEM(one, f32),
                pltpu.VMEM(slot, f32), pltpu.VMEM(slot, f32),
                pltpu.VMEM(one, f32), pltpu.VMEM(one, f32), pltpu.VMEM(one, f32),
                pltpu.SMEM((2, levels), f32), pltpu.SMEM(mode_counts.shape, jnp.int32),
                pltpu.SMEM((windows,), jnp.int32), pltpu.SMEM((windows,), f32),
                dma((6,)), dma((2,)), dma((2,)), dma((13, nc)), dma((13, nc)), regular, regular,
            ],
            compiler_params=pltpu.CompilerParams(collective_id=0, has_side_effects=True),
        )(ctrl, pert, vertical_modes.T, mode_counts, slot_index, blend_weight)
        out = pl.pallas_call(
            blend_kernel,
            out_shape=jax.ShapeDtypeStruct((windows, levels, 8, 128), f32),
            in_specs=[vmem, vmem],
            out_specs=hbm,
            scratch_shapes=[pltpu.VMEM((windows, levels, 8, 128), f32), dma((windows,))],
        )(*(pltpu.with_memory_space_constraint(x, pltpu.VMEM) for x in (gath, scale)))
        out = out.reshape(windows, levels, 2, 4, 128)
        return jnp.swapaxes(out, -3, -2).reshape(windows, levels, 4, 256)

    return jax.shard_map(
        per_device,
        mesh=mesh,
        in_specs=(
            P("mem", None, "tile", None), P(), P("tile"),
            P("mem", "tm", None, "tile", None), P("tm"), P("tm"),
        ),
        out_specs=P("tm", None, "tile", None),
        check_vma=False,
    )
```

time: 43.8 us -> 33.9 us (0.77)
  the two profiles are of different devices: /device:TPU:8 before, /device:TPU:480 now
where the time goes in v2:
time: 33.9 us; the launch traced here: 33.5 us
  Pallas kernels  33.5 us (99%)
    pallas_call x1, Pallas kernels, per_device(): pl.pallas_call(functools.partial(kernel, n_tm, n_mem, n_tile, members, wi...  32.5 us
    pallas_call x1, Pallas kernels, per_device(): pl.pallas_call(blend_kernel, out_shape=jax.ShapeDtypeStruct((windows, lev...  0.94 us

profile of v2, /device:TPU:480, one launch (start us, length us, event | category | flops | bytes accessed | tf_op | source)
XLA Modules:
  0.0 33.5 jit_solution(9082224338224496548)
XLA Ops:
  0.0 32.5 %shard_map.64 = (f32[4,4,3,4,8,128]{5,4,3,2,1,0:T(8,128)S(1)}, f32[3,2,8,128]{3,2,1,0:T(8,128)S(1)}) custom-call(f32[160,128]{1,0:T(8,128)} %bitcast.17, bf16[10,2,32,16,128]{4,3,2,1,0:T(8,128)(2,1)} %bitcast.16, f32[2,64]{1,0:T(2,128)} %bitcast.18, s32[4]{0:T(128)} %counts_hbm.1, s32[3]{0:T(128)} %index_hbm.1, f32[3]{0:T(128)} %weight_hbm.1), custom_call_target="tpu_custom_call" | custom-call | tf_op jit(solution)/shard_map/pallas_call | solution.py:352
  32.5 0.9 %shard_map.65 = f32[3,64,8,128]{3,2,1,0:T(8,128)} custom-call(f32[4,4,3,4,8,128]{5,4,3,2,1,0:T(8,128)S(1)} %get-tuple-element.7.gath, f32[3,2,8,128]{3,2,1,0:T(8,128)S(1)} %get-tuple-element.8.scale), custom_call_target="tpu_custom_call" | custom-call | tf_op jit(solution)/shard_map/pallas_call | solution.py:374

commit v3 on v2

--- a/solution.py
+++ b/solution.py
@@ -11,7 +11,8 @@
 
 SMOOTH = 4
 DIFFUSION = 0.24
-CHUNKS = 4
+CHUNKS = 8
+DIRECT = 3
 MESH = pl.DeviceIdType.MESH
 
 
@@ -54,9 +55,9 @@
     n_tm, n_mem, n_tile, members, windows,
     ctrl, pert_hbm, modes_hbm, counts_hbm, index_hbm, weight_hbm,
     gath, scale,
-    halo, pert, f_ref, far, near_r, near_l, mail_a, mail_b, mail_r, mail_l,
+    halo, pert, f_ref, far, near, mail_far, mail,
     za_out, za_in, zb_in, modes, counts, slot_index, weight,
-    load_sems, halo_send, halo_recv, send, recv, ready_next, ready_back,
+    load_sems, halo_sems, send, recv, recv_all, ready_next, ready_back,
 ):
     t, m = lax.axis_index("tm"), lax.axis_index("mem")
     tile = lax.axis_index("tile")
@@ -66,18 +67,26 @@
     quarter_pairs = nc * pairs
     norm = 1.0 / math.sqrt(members * n_mem - 1)
 
-    tile_r, tile_l = lax.rem(tile + 1, n_tile), lax.rem(tile + n_tile - 1, n_tile)
     mem_r, mem_l = lax.rem(m + 1, n_mem), lax.rem(m + n_mem - 1, n_mem)
     mem_f = lax.rem(m + 2, n_mem)
     tm_r, tm_l = lax.rem(t + 1, n_tm), lax.rem(t + n_tm - 1, n_tm)
     right, left, across = {"mem": mem_r}, {"mem": mem_l}, {"mem": mem_f}
     onward, back = {"tm": tm_r}, {"tm": tm_l}
+    run = n_tile // 4
+    place = lax.rem(tile, run)
+    tile_r, tile_l = lax.rem(tile + 1, n_tile), lax.rem(tile + n_tile - 1, n_tile)
+    head, tail = place == 0, place == run - 1
+    low, high = t == 0, t == n_tm - 1
+    step_r = jnp.where(tail & jnp.logical_not(high), tm_r, t)
+    step_l = jnp.where(head & jnp.logical_not(low), tm_l, t)
+    next_tile = {"tm": step_r, "tile": tile_r}
+    last_tile = {"tm": step_l, "tile": tile_l}
 
     def signal(sem, device):
         pl.semaphore_signal(sem, inc=1, device_id=device, device_id_type=MESH)
 
     barrier = pltpu.get_barrier_semaphore()
-    partners = ({"tile": tile_r}, {"tile": tile_l}, right, left, across)
+    partners = (next_tile, last_tile, right, left, across)
     for partner in partners:
         signal(barrier, partner)
 
@@ -101,6 +110,8 @@
     with scope("barrier"):
         loads[0].wait()
         extra = jnp.where(t == 0, 0, jnp.where(t == 2, 2, 1))
+        extra += jnp.where((low & tail) | (high & head), 1, 0)
+        extra -= jnp.where((low & head) | (high & tail), 1, 0)
         pl.semaphore_wait(barrier, len(partners) + extra)
 
     def remote(src, dst, s, r, device):
@@ -109,10 +120,35 @@
             device_id=device, device_id_type=MESH,
         )
 
-    to_right = remote(halo.at[1], halo.at[0], halo_send.at[0], halo_recv.at[0], {"tile": tile_r})
-    to_left = remote(halo.at[1], halo.at[2], halo_send.at[1], halo_recv.at[1], {"tile": tile_l})
-    to_right.start()
-    to_left.start()
+    def to_right(device):
+        return remote(halo.at[1], halo.at[0], halo_sems.at[0], halo_sems.at[1], device)
+
+    def to_left(device):
+        return remote(halo.at[1], halo.at[2], halo_sems.at[2], halo_sems.at[3], device)
+
+    def to_both_tm(copy):
+        return remote(halo.at[1], copy[0], halo_sems.at[4], copy[1], copy[2])
+
+    wrap_r = to_both_tm((halo.at[0], halo_sems.at[1], {"tile": tile_r}))
+    wrap_l = to_both_tm((halo.at[2], halo_sems.at[3], {"tile": tile_l}))
+    sends_r = jnp.logical_not(high & tail)
+    sends_l = jnp.logical_not(low & head)
+
+    @pl.when(sends_r)
+    def _():
+        to_right(next_tile).start()
+
+    @pl.when(sends_l)
+    def _():
+        to_left(last_tile).start()
+
+    @pl.when(low & tail)
+    def _():
+        wrap_r.start()
+
+    @pl.when(high & head)
+    def _():
+        wrap_l.start()
 
     @pl.when((t == 1) | (t == 2))
     def _():
@@ -129,9 +165,18 @@
         later = slot_index[w] - 2 * t == 1
         scale[w, 0] = jnp.full((8, 128), jnp.where(later, 1.0, b), jnp.float32)
         scale[w, 1] = jnp.full((8, 128), jnp.where(later, b, 0.0), jnp.float32)
+
+    @pl.when(t == 0)
+    def _():
+        def clear(i, carry):
+            gath[i // nc, lax.rem(i, nc), 2] = jnp.zeros_like(za_out[0])
+            return carry
+
+        lax.fori_loop(0, n_mem * nc, clear, 0)
+
     with scope("halo"):
-        to_right.wait()
-        to_left.wait()
+        to_right(next_tile).wait_recv()
+        to_left(last_tile).wait_recv()
 
     with scope("smooth"):
         fields = 2 * members
@@ -163,149 +208,199 @@
         else:
             lax.fori_loop(0, pairs, body, 0)
 
-    def channel(k, chunk, src, dst, device):
-        return remote(src, dst, send.at[k, chunk], recv.at[k, chunk], device)
+    def channel(k, c, src, dst, device):
+        arrived = recv_all.at[k - 5] if k >= 5 else recv.at[k, c]
+        return remote(src, dst, send.at[k], arrived, device)
+
+    def arrive(k, c, size):
+        channel(k, c, size, size, right).wait_recv()
+
+    def sent(k, size):
+        channel(k, 0, size, size, right).wait_send()
 
     def both(ref):
         return ref.at[pl.ds(0, 2)]
 
-    far_r = [channel(0, c, far.at[c, 0], mail_a.at[c], right) for c in range(nc)]
-    far_l = [channel(1, c, far.at[c, 1], mail_b.at[c], left) for c in range(nc)]
-    sum_r = [channel(2, c, near_r.at[c], mail_r.at[c], right) for c in range(nc)]
-    sum_l = [channel(3, c, near_l.at[c], mail_l.at[c], left) for c in range(nc)]
-    chain = [channel(4, c, za_out.at[c], za_in.at[c], onward) for c in range(nc)]
-    around = [channel(5, c, za_out.at[c], zb_in.at[c], back) for c in range(nc)]
-    relay = [channel(5, c, zb_in.at[c], zb_in.at[c], back) for c in range(nc)]
-    slots_r = [channel(6, c, both(gath.at[m, c]), both(gath.at[m, c]), right) for c in range(nc)]
-    slots_l = [channel(7, c, both(gath.at[m, c]), both(gath.at[m, c]), left) for c in range(nc)]
-    pass_r = [channel(8, c, gath.at[mem_l, c, 0], gath.at[mem_l, c, 0], right) for c in range(nc)]
-    pass_l = [channel(9, c, gath.at[mem_r, c, 1], gath.at[mem_r, c, 1], left) for c in range(nc)]
-    early_r = [channel(10, c, gath.at[m, c, 2], gath.at[m, c, 2], right) for c in range(nc)]
-    early_l = [channel(11, c, gath.at[m, c, 2], gath.at[m, c, 2], left) for c in range(nc)]
-    early_f = [channel(12, c, gath.at[m, c, 2], gath.at[m, c, 2], across) for c in range(nc)]
+    def chain(c):
+        return channel(2, c, za_out.at[c], za_in.at[c], onward)
+
+    def around(c):
+        return channel(3, c, za_out.at[c], zb_in.at[c], back)
+
+    def relay(c):
+        return channel(3, c, zb_in.at[c], zb_in.at[c], back)
+
+    direct = range(DIRECT)
+    ringed = range(DIRECT, nc)
+
+    def send_near(c, side):
+        channel(1, c, near.at[c, side], mail.at[c, side], (right, left)[side]).start()
 
     with scope("far"):
-        for c in range(nc):
+        for c in direct:
             part(mem_f, c, far.at[c])
-            far_r[c].start()
-            far_l[c].start()
+            remote(far.at[c], mail.at[c, 2], send.at[0], recv.at[1, c], across).start()
+            part(mem_r, c, near.at[c, 0])
+            send_near(c, 0)
+            part(mem_l, c, near.at[c, 1])
+            send_near(c, 1)
+        for c in ringed:
+            part(mem_f, c, far.at[c])
+            channel(0, c, far.at[c, 0], mail_far.at[c, 0], right).start()
+            channel(0, c, far.at[c, 1], mail_far.at[c, 1], left).start()
     with scope("near"):
-        for c in range(nc):
-            part(mem_r, c, near_r.at[c])
-            part(mem_l, c, near_l.at[c])
+        for c in ringed:
+            part(mem_r, c, near.at[c, 0])
+            part(mem_l, c, near.at[c, 1])
         for c in range(nc):
             part(m, c, gath.at[m, c])
 
-    for c in range(nc):
-        with scope(f"A{c}"):
-            far_r[c].wait_recv()
-            near_r[c, 0] += mail_a[c]
-            sum_r[c].start()
-            far_l[c].wait_recv()
-            near_l[c, 1] += mail_b[c]
-            sum_l[c].start()
-
-    with scope("R"):
-        @pl.when(t < 2)
-        def _():
-            pl.semaphore_wait(ready_next, 1)
-
-        @pl.when((t == 0) | (t == 3))
-        def _():
-            pl.semaphore_wait(ready_back, 1)
-
-    for c in range(nc):
-        with scope(f"B{c}"):
-            sum_r[c].wait_recv()
-            sum_l[c].wait_recv()
-            for level in range(lc):
-                total = None
-                for s in range(2):
-                    value = gath[m, c, s, level] + (mail_r[c, s, level] + mail_l[c, s, level])
-                    gath[m, c, s, level] = value
-                    total = value if s == 0 else total + value
-                za_out[c, level] = total
-
+    def step_a(c):
+        arrive(0, c, mail_far.at[c])
+        near[c, 0, 0] += mail_far[c, 0]
+        send_near(c, 0)
+        near[c, 1, 1] += mail_far[c, 1]
+        send_near(c, 1)
+
+    def step_b(c):
+        sources = 3 if c < DIRECT else 2
+        arrive(1, c, mail.at[c, pl.ds(0, sources)])
+        for level in range(lc):
+            total = None
+            for s in range(2):
+                value = mail[c, 0, s, level] + mail[c, 1, s, level]
+                if sources == 3:
+                    value = value + mail[c, 2, s, level]
+                value = gath[m, c, s, level] + value
+                gath[m, c, s, level] = value
+                total = value if s == 0 else total + value
+            za_out[c, level] = total
+
+        if c == 0:
             @pl.when(t < 2)
             def _():
-                chain[c].start()
-
-            @pl.when(t == 0)
+                pl.semaphore_wait(ready_next, 1)
+
+            @pl.when((t == 0) | (t == 3))
             def _():
-                around[c].start()
-
-            slots_r[c].start()
-            slots_l[c].start()
-
-    for c in range(nc):
-        with scope(f"Z{c}"):
-            @pl.when(t == 2)
-            def _():
-                chain[c].wait_recv()
-                za_out[c] += za_in[c]
-                chain[c].start()
-
-            @pl.when(t == 3)
-            def _():
-                around[c].wait_recv()
-                relay[c].start()
-        with scope(f"D{c}"):
-            slots_r[c].wait_recv()
-            pass_r[c].start()
-            slots_l[c].wait_recv()
-            pass_l[c].start()
-
-    for c in range(nc):
-        with scope(f"E{c}"):
-            @pl.when(t == 0)
-            def _():
-                gath[m, c, 2] = jnp.zeros_like(gath[m, c, 2])
-
-            @pl.when(t == 1)
-            def _():
-                chain[c].wait_recv()
-                gath[m, c, 2] = za_in[c]
-
-            @pl.when(t == 2)
-            def _():
-                relay[c].wait_recv()
-                gath[m, c, 2] = za_in[c] + zb_in[c]
-
-            @pl.when(t == 3)
-            def _():
-                chain[c].wait_recv()
-                gath[m, c, 2] = za_in[c] + zb_in[c]
-
-            early_r[c].start()
-            early_l[c].start()
-            early_f[c].start()
+                pl.semaphore_wait(ready_back, 1)
+
+        @pl.when(t < 2)
+        def _():
+            chain(c).start()
+
+        @pl.when(t == 0)
+        def _():
+            around(c).start()
+
+    def step_g(c):
+        for device in (right, left):
+            channel(4, c, both(gath.at[m, c]), both(gath.at[m, c]), device).start()
+
+    def step_z2(c):
+        chain(c).wait_recv()
+        za_out[c] += za_in[c]
+        chain(c).start()
+
+    def step_z3(c):
+        around(c).wait_recv()
+        relay(c).start()
+
+    def step_d(c):
+        arrive(4, c, near.at[c])
+        channel(5, c, gath.at[mem_l, c, 0], gath.at[mem_l, c, 0], right).start()
+        channel(5, c, gath.at[mem_r, c, 1], gath.at[mem_r, c, 1], left).start()
+
+    def early_1(c):
+        chain(c).wait_recv()
+        gath[m, c, 2] = za_in[c]
+
+    def early_2(c):
+        relay(c).wait_recv()
+        gath[m, c, 2] = za_in[c] + zb_in[c]
+
+    def early_3(c):
+        chain(c).wait_recv()
+        gath[m, c, 2] = za_in[c] + zb_in[c]
+
+    def step_e(c, early):
+        early(c)
+        for device in (across, right, left):
+            channel(6, c, gath.at[m, c, 2], gath.at[m, c, 2], device).start()
+
+    def run(steps):
+        for step, *args in steps:
+            with scope(f"{step.__name__.replace("step_","").upper()[0]}{args[0]}"):
+                step(*args)
+
+    every = range(nc)
+    first = [(step_a, c) for c in ringed[:1]]
+    for k in range(max(DIRECT, nc - DIRECT - 1)):
+        if DIRECT + 1 + k < nc:
+            first.append((step_a, DIRECT + 1 + k))
+        if k < DIRECT:
+            first.append((step_b, k))
+    run(first)
+
+    @pl.when(t < 2)
+    def _():
+        run([(step_b, c) for c in ringed] + [(step_g, c) for c in every] + [(step_d, c) for c in every])
+
+    @pl.when(t == 1)
+    def _():
+        run([(step_e, c, early_1) for c in every])
+
+    @pl.when(t == 2)
+    def _():
+        run([(step_z2, c) for c in direct] + [(step_b, c) for c in ringed])
+        run([(step_g, c) for c in every] + [(step_z2, c) for c in ringed])
+        for c in every:
+            run([(step_e, c, early_2), (step_d, c)])
+
+    @pl.when(t == 3)
+    def _():
+        run([(step_z3, c) for c in direct])
+        for c in ringed:
+            run([(step_b, c), (step_z3, c)])
+        run([(step_g, c) for c in every] + [(step_d, c) for c in every])
+        run([(step_e, c, early_3) for c in every])
 
     with scope("P"):
-        for c in range(nc):
-            pass_r[c].wait_recv()
-            pass_l[c].wait_recv()
-
-    for c in range(nc):
-        with scope(f"H{c}"):
-            early_r[c].wait_recv()
-            early_l[c].wait_recv()
-            early_f[c].wait_recv()
-
-    for group in (far_r, far_l, sum_r, sum_l, slots_r, slots_l, pass_r, pass_l, early_r, early_l, early_f):
-        for copy in group:
-            copy.wait_send()
-    for c in range(nc):
+        arrive(5, 0, far)
+    with scope("H"):
+        @pl.when(t > 0)
+        def _():
+            arrive(6, 0, gath.at[0])
+
+    with scope("W"):
+        @pl.when(sends_r)
+        def _():
+            to_right(next_tile).wait_send()
+
+        @pl.when(sends_l)
+        def _():
+            to_left(last_tile).wait_send()
+
+        @pl.when((low & tail) | (high & head))
+        def _():
+            wrap_r.wait_send()
+
+        sent(0, far)
+        sent(1, near)
+        sent(4, near)
+        sent(5, far)
+
         @pl.when(t < 3)
         def _():
-            chain[c].wait_send()
-
-        @pl.when(t == 0)
-        def _():
-            around[c].wait_send()
-
-        @pl.when(t == 3)
-        def _():
-            relay[c].wait_send()
+            sent(2, za_out)
+
+        @pl.when((t == 0) | (t == 3))
+        def _():
+            sent(3, za_out)
+
+        @pl.when(t > 0)
+        def _():
+            sent(6, gath.at[0])
 
 
 def blend_kernel(gath, scale, out, block, sems):
@@ -361,13 +456,12 @@
                 pltpu.VMEM((3, rows, 128), f32),
                 pltpu.VMEM(pert.shape, jnp.bfloat16),
                 pltpu.VMEM((rows, 128), f32),
-                pltpu.VMEM(slot, f32), pltpu.VMEM(slot, f32), pltpu.VMEM(slot, f32),
-                pltpu.VMEM(one, f32), pltpu.VMEM(one, f32),
-                pltpu.VMEM(slot, f32), pltpu.VMEM(slot, f32),
+                pltpu.VMEM(slot, f32), pltpu.VMEM((nc, 2, *slot[1:]), f32),
+                pltpu.VMEM(slot, f32), pltpu.VMEM((nc, 3, *slot[1:]), f32),
                 pltpu.VMEM(one, f32), pltpu.VMEM(one, f32), pltpu.VMEM(one, f32),
                 pltpu.SMEM((2, levels), f32), pltpu.SMEM(mode_counts.shape, jnp.int32),
                 pltpu.SMEM((windows,), jnp.int32), pltpu.SMEM((windows,), f32),
-                dma((6,)), dma((2,)), dma((2,)), dma((13, nc)), dma((13, nc)), regular, regular,
+                dma((6,)), dma((5,)), dma((7,)), dma((5, nc)), dma((2,)), regular, regular,
             ],
             compiler_params=pltpu.CompilerParams(collective_id=0, has_side_effects=True),
         )(ctrl, pert, vertical_modes.T, mode_counts, slot_index, blend_weight)

time: 33.9 us -> 32.4 us (0.956)
  Pallas kernels: 33.5 us -> 32.2 us
    pallas_call x1, Pallas kernels: 32.5 us -> 31.3 us  [per_device(): pl.pallas_call(functools.partial(kernel, n_tm, n_mem, n_tile, members, wi...]
where the time goes in v3:
time: 32.4 us; the launch traced here: 32.3 us
  Pallas kernels  32.2 us (99%)
    pallas_call x1, Pallas kernels, per_device(): pl.pallas_call(functools.partial(kernel, n_tm, n_mem, n_tile, members, wi...  31.3 us
    pallas_call x1, Pallas kernels, per_device(): pl.pallas_call(blend_kernel, out_shape=jax.ShapeDtypeStruct((windows, lev...  0.94 us

profile of v3, /device:TPU:480, one launch (start us, length us, event | category | flops | bytes accessed | tf_op | source)
XLA Modules:
  0.0 32.3 jit_solution(16838128824799979097)
XLA Ops:
  0.0 31.3 %shard_map.64 = (f32[4,8,3,2,8,128]{5,4,3,2,1,0:T(8,128)S(1)}, f32[3,2,8,128]{3,2,1,0:T(8,128)S(1)}) custom-call(f32[160,128]{1,0:T(8,128)} %bitcast.17, bf16[10,2,32,16,128]{4,3,2,1,0:T(8,128)(2,1)} %bitcast.16, f32[2,64]{1,0:T(2,128)} %bitcast.18, s32[4]{0:T(128)} %counts_hbm.1, s32[3]{0:T(128)} %index_hbm.1, f32[3]{0:T(128)} %weight_hbm.1), custom_call_target="tpu_custom_call" | custom-call | tf_op jit(solution)/shard_map/pallas_call | solution.py:447
  31.3 0.9 %shard_map.65 = f32[3,64,8,128]{3,2,1,0:T(8,128)} custom-call(f32[4,8,3,2,8,128]{5,4,3,2,1,0:T(8,128)S(1)} %get-tuple-element.7.gath, f32[3,2,8,128]{3,2,1,0:T(8,128)S(1)} %get-tuple-element.8.scale), custom_call_target="tpu_custom_call" | custom-call | tf_op jit(solution)/shard_map/pallas_call | solution.py:468

commit v4 on v3

--- a/solution.py
+++ b/solution.py
@@ -12,6 +12,7 @@
 SMOOTH = 4
 DIFFUSION = 0.24
 CHUNKS = 8
+HOP = 1
 DIRECT = 3
 MESH = pl.DeviceIdType.MESH
 
@@ -56,8 +57,8 @@
     ctrl, pert_hbm, modes_hbm, counts_hbm, index_hbm, weight_hbm,
     gath, scale,
     halo, pert, f_ref, far, near, mail_far, mail,
-    za_out, za_in, zb_in, modes, counts, slot_index, weight,
-    load_sems, halo_sems, send, recv, recv_all, ready_next, ready_back,
+    za_out, za_in, zb_in, zc_in, modes, counts, slot_index, weight,
+    load_sems, halo_sems, send, recv, ready_next, ready_back,
 ):
     t, m = lax.axis_index("tm"), lax.axis_index("mem")
     tile = lax.axis_index("tile")
@@ -76,8 +77,8 @@
     place = lax.rem(tile, run)
     tile_r, tile_l = lax.rem(tile + 1, n_tile), lax.rem(tile + n_tile - 1, n_tile)
     head, tail = place == 0, place == run - 1
-    low, high = t == 0, t == n_tm - 1
-    step_r = jnp.where(tail & jnp.logical_not(high), tm_r, t)
+    low, high, odd = t == 0, t == n_tm - 1, lax.rem(t, 2) == 1
+    step_r = jnp.where(tail & jnp.logical_not(odd), tm_r, t)
     step_l = jnp.where(head & jnp.logical_not(low), tm_l, t)
     next_tile = {"tm": step_r, "tile": tile_r}
     last_tile = {"tm": step_l, "tile": tile_l}
@@ -110,8 +111,8 @@
     with scope("barrier"):
         loads[0].wait()
         extra = jnp.where(t == 0, 0, jnp.where(t == 2, 2, 1))
-        extra += jnp.where((low & tail) | (high & head), 1, 0)
-        extra -= jnp.where((low & head) | (high & tail), 1, 0)
+        extra += jnp.where((low & tail) | (odd & head), 1, 0)
+        extra -= jnp.where((jnp.logical_not(odd) & head) | (high & tail), 1, 0)
         pl.semaphore_wait(barrier, len(partners) + extra)
 
     def remote(src, dst, s, r, device):
@@ -132,11 +133,12 @@
     wrap_r = to_both_tm((halo.at[0], halo_sems.at[1], {"tile": tile_r}))
     wrap_l = to_both_tm((halo.at[2], halo_sems.at[3], {"tile": tile_l}))
     sends_r = jnp.logical_not(high & tail)
-    sends_l = jnp.logical_not(low & head)
+    sends_l = jnp.logical_not(head & jnp.logical_not(odd))
+    right_tile = {"tm": jnp.where(tail, tm_r, t), "tile": tile_r}
 
     @pl.when(sends_r)
     def _():
-        to_right(next_tile).start()
+        to_right(right_tile).start()
 
     @pl.when(sends_l)
     def _():
@@ -146,7 +148,7 @@
     def _():
         wrap_r.start()
 
-    @pl.when(high & head)
+    @pl.when(odd & head)
     def _():
         wrap_l.start()
 
@@ -169,7 +171,7 @@
     @pl.when(t == 0)
     def _():
         def clear(i, carry):
-            gath[i // nc, lax.rem(i, nc), 2] = jnp.zeros_like(za_out[0])
+            gath[i // nc, lax.rem(i, nc), 2] = jnp.zeros((lc, 8, 128), jnp.float32)
             return carry
 
         lax.fori_loop(0, n_mem * nc, clear, 0)
@@ -208,27 +210,45 @@
         else:
             lax.fori_loop(0, pairs, body, 0)
 
+    late = place >= run - 2
+
+    half = nc // 2
+    hops = nc * lc // HOP
+    bases = (-DIRECT, nc - DIRECT, 2 * nc - DIRECT, 2 * nc - DIRECT + hops)
+    bases += (bases[3] + half, bases[3] + half + 2, bases[3] + half + 3)
+    bases += (bases[6] + 1,)
+    shares = (1, 1, 1, 2, half, nc, nc, 2)
+
     def channel(k, c, src, dst, device):
-        arrived = recv_all.at[k - 5] if k >= 5 else recv.at[k, c]
-        return remote(src, dst, send.at[k], arrived, device)
+        return remote(src, dst, send.at[k], recv.at[bases[k] + c // shares[k]], device)
 
     def arrive(k, c, size):
         channel(k, c, size, size, right).wait_recv()
 
     def sent(k, size):
-        channel(k, 0, size, size, right).wait_send()
+        remote(size, size, send.at[k], recv.at[0], right).wait_send()
 
     def both(ref):
         return ref.at[pl.ds(0, 2)]
 
-    def chain(c):
-        return channel(2, c, za_out.at[c], za_in.at[c], onward)
+    def units(c):
+        return [u for u in range(nc * lc // HOP) if c * lc < (u + 1) * HOP <= (c + 1) * lc]
+
+    def chain(u):
+        own = pl.ds(u * HOP, HOP)
+        return channel(2, u, za_out.at[own], za_in.at[own], onward)
 
     def around(c):
-        return channel(3, c, za_out.at[c], zb_in.at[c], back)
+        two = pl.ds((c - 1) * lc, 2 * lc)
+        return channel(3, c, za_out.at[two], zb_in.at[two], back)
 
     def relay(c):
-        return channel(3, c, zb_in.at[c], zb_in.at[c], back)
+        two = pl.ds((c - 1) * lc, 2 * lc)
+        return channel(3, c, zb_in.at[two], zb_in.at[two], back)
+
+    def bypass(c):
+        two = pl.ds((c - 1) * lc, 2 * lc)
+        return channel(7, c, zb_in.at[two], zc_in.at[two], back)
 
     direct = range(DIRECT)
     ringed = range(DIRECT, nc)
@@ -237,17 +257,17 @@
         channel(1, c, near.at[c, side], mail.at[c, side], (right, left)[side]).start()
 
     with scope("far"):
+        for c in ringed:
+            part(mem_f, c, far.at[c])
+            channel(0, c, far.at[c, 0], mail_far.at[c, 0], right).start()
+            channel(0, c, far.at[c, 1], mail_far.at[c, 1], left).start()
         for c in direct:
             part(mem_f, c, far.at[c])
-            remote(far.at[c], mail.at[c, 2], send.at[0], recv.at[1, c], across).start()
+            remote(far.at[c], mail.at[c, 2], send.at[0], recv.at[bases[1] + c], across).start()
             part(mem_r, c, near.at[c, 0])
             send_near(c, 0)
             part(mem_l, c, near.at[c, 1])
             send_near(c, 1)
-        for c in ringed:
-            part(mem_f, c, far.at[c])
-            channel(0, c, far.at[c, 0], mail_far.at[c, 0], right).start()
-            channel(0, c, far.at[c, 1], mail_far.at[c, 1], left).start()
     with scope("near"):
         for c in ringed:
             part(mem_r, c, near.at[c, 0])
@@ -274,7 +294,7 @@
                 value = gath[m, c, s, level] + value
                 gath[m, c, s, level] = value
                 total = value if s == 0 else total + value
-            za_out[c, level] = total
+            za_out[c * lc + level] = total
 
         if c == 0:
             @pl.when(t < 2)
@@ -285,50 +305,74 @@
             def _():
                 pl.semaphore_wait(ready_back, 1)
 
-        @pl.when(t < 2)
-        def _():
-            chain(c).start()
-
-        @pl.when(t == 0)
-        def _():
-            around(c).start()
+        @pl.when((t < 2) | (late & (t == 2)))
+        def _():
+            for u in units(c):
+                chain(u).start()
+
+        if c % 2 == 1:
+            @pl.when((t == 0) | (late & (t == 1)))
+            def _():
+                around(c).start()
 
     def step_g(c):
+        own = both(gath.at[m, c])
         for device in (right, left):
-            channel(4, c, both(gath.at[m, c]), both(gath.at[m, c]), device).start()
+            channel(4, c, own, own, device).start()
+        if c >= half:
+            remote(own, own, send.at[5], recv.at[bases[4] + 1], across).start()
 
     def step_z2(c):
-        chain(c).wait_recv()
-        za_out[c] += za_in[c]
-        chain(c).start()
+        for u in units(c):
+            chain(u).wait_recv()
+            for level in range(u * HOP, (u + 1) * HOP):
+                za_out[level] += za_in[level]
+            chain(u).start()
 
     def step_z3(c):
-        around(c).wait_recv()
-        relay(c).start()
-
-    def step_d(c):
-        arrive(4, c, near.at[c])
-        channel(5, c, gath.at[mem_l, c, 0], gath.at[mem_l, c, 0], right).start()
-        channel(5, c, gath.at[mem_r, c, 1], gath.at[mem_r, c, 1], left).start()
-
-    def early_1(c):
-        chain(c).wait_recv()
-        gath[m, c, 2] = za_in[c]
-
-    def early_2(c):
-        relay(c).wait_recv()
-        gath[m, c, 2] = za_in[c] + zb_in[c]
-
-    def early_3(c):
-        chain(c).wait_recv()
-        gath[m, c, 2] = za_in[c] + zb_in[c]
+        if c % 2 == 1:
+            around(c).wait_recv()
+            relay(c).start()
+
+    def step_d():
+        arrive(4, 0, near.at[pl.ds(0, half)])
+        for c in range(half):
+            channel(5, 0, gath.at[mem_l, c, 0], gath.at[mem_l, c, 0], right).start()
+            channel(5, 0, gath.at[mem_r, c, 1], gath.at[mem_r, c, 1], left).start()
+
+    def early_1(level):
+        return za_in[level]
+
+    def early_23(level):
+        return za_in[level] + zb_in[level]
 
     def step_e(c, early):
-        early(c)
+        def come():
+            for u in units(c):
+                chain(u).wait_recv()
+
+        if early is early_23 and c % 2 == 0:
+            @pl.when(t == 2)
+            def _():
+                relay(c + 1).wait_recv()
+
+            @pl.when(late & (t == 3))
+            def _():
+                bypass(c + 1).wait_recv()
+
+        pl.when((t != 2) | late)(come)
+        for level in range(lc):
+            gath[m, c, 2, level] = early(c * lc + level)
+        if early is early_23:
+            @pl.when(late & (t == 3))
+            def _():
+                for level in range(lc):
+                    gath[m, c, 2, level] += zc_in[c * lc + level]
+
         for device in (across, right, left):
             channel(6, c, gath.at[m, c, 2], gath.at[m, c, 2], device).start()
 
-    def run(steps):
+    def play(steps):
         for step, *args in steps:
             with scope(f"{step.__name__.replace("step_","").upper()[0]}{args[0]}"):
                 step(*args)
@@ -340,33 +384,57 @@
             first.append((step_a, DIRECT + 1 + k))
         if k < DIRECT:
             first.append((step_b, k))
-    run(first)
-
-    @pl.when(t < 2)
-    def _():
-        run([(step_b, c) for c in ringed] + [(step_g, c) for c in every] + [(step_d, c) for c in every])
+    play(first)
+
+    def rest(also=None):
+        for c in ringed:
+            play([(step_b, c)])
+            if also is not None:
+                play([(also, c)])
+            play([(step_g, k) for k in (range(DIRECT + 1) if c == DIRECT else (c,))])
+
+    @pl.when(t == 0)
+    def _():
+        rest()
+        step_d()
+
+        @pl.when(late)
+        def _():
+            for c in range(1, nc, 2):
+                around(c).wait_recv()
+                bypass(c).start()
 
     @pl.when(t == 1)
     def _():
-        run([(step_e, c, early_1) for c in every])
+        play([(step_b, c) for c in ringed] + [(step_g, c) for c in every])
+        step_d()
+        play([(step_e, c, early_1) for c in every])
+
+    @pl.when((t == 2) & jnp.logical_not(late))
+    def _():
+        play([(step_z2, c) for c in direct])
+        rest(step_z2)
+
+    @pl.when((t == 2) & late)
+    def _():
+        rest()
 
     @pl.when(t == 2)
     def _():
-        run([(step_z2, c) for c in direct] + [(step_b, c) for c in ringed])
-        run([(step_g, c) for c in every] + [(step_z2, c) for c in ringed])
-        for c in every:
-            run([(step_e, c, early_2), (step_d, c)])
+        play([(step_e, c, early_23) for c in range(half)])
+        step_d()
+        play([(step_e, c, early_23) for c in range(half, nc)])
 
     @pl.when(t == 3)
     def _():
-        run([(step_z3, c) for c in direct])
-        for c in ringed:
-            run([(step_b, c), (step_z3, c)])
-        run([(step_g, c) for c in every] + [(step_d, c) for c in every])
-        run([(step_e, c, early_3) for c in every])
+        play([(step_z3, c) for c in direct])
+        rest(step_z3)
+        step_d()
+        play([(step_e, c, early_23) for c in every])
 
     with scope("P"):
-        arrive(5, 0, far)
+        arrive(4, half, mail.at[pl.ds(0, half)])
+        arrive(5, 0, far.at[pl.ds(0, half)])
     with scope("H"):
         @pl.when(t > 0)
         def _():
@@ -375,13 +443,13 @@
     with scope("W"):
         @pl.when(sends_r)
         def _():
-            to_right(next_tile).wait_send()
+            to_right(right_tile).wait_send()
 
         @pl.when(sends_l)
         def _():
             to_left(last_tile).wait_send()
 
-        @pl.when((low & tail) | (high & head))
+        @pl.when((low & tail) | (odd & head))
         def _():
             wrap_r.wait_send()
 
@@ -397,6 +465,14 @@
         @pl.when((t == 0) | (t == 3))
         def _():
             sent(3, za_out)
+
+        @pl.when(late & (t == 1))
+        def _():
+            sent(3, za_out)
+
+        @pl.when(late & (t == 0))
+        def _():
+            sent(7, za_out)
 
         @pl.when(t > 0)
         def _():
@@ -439,7 +515,7 @@
         lc = levels // n_mem // nc
         f32 = jnp.float32
         slot = (nc, slots, lc, 8, 128)
-        one = (nc, lc, 8, 128)
+        one = (nc * lc, 8, 128)
         vmem = pl.BlockSpec(memory_space=pltpu.VMEM)
         hbm = pl.BlockSpec(memory_space=pl.ANY)
         dma = pltpu.SemaphoreType.DMA
@@ -458,10 +534,10 @@
                 pltpu.VMEM((rows, 128), f32),
                 pltpu.VMEM(slot, f32), pltpu.VMEM((nc, 2, *slot[1:]), f32),
                 pltpu.VMEM(slot, f32), pltpu.VMEM((nc, 3, *slot[1:]), f32),
-                pltpu.VMEM(one, f32), pltpu.VMEM(one, f32), pltpu.VMEM(one, f32),
+                pltpu.VMEM(one, f32), pltpu.VMEM(one, f32), pltpu.VMEM(one, f32), pltpu.VMEM(one, f32),
                 pltpu.SMEM((2, levels), f32), pltpu.SMEM(mode_counts.shape, jnp.int32),
                 pltpu.SMEM((windows,), jnp.int32), pltpu.SMEM((windows,), f32),
-                dma((6,)), dma((5,)), dma((7,)), dma((5, nc)), dma((2,)), regular, regular,
+                dma((6,)), dma((5,)), dma((8,)), dma((2 * nc - DIRECT + nc * lc // HOP + nc + 4,)), regular, regular,
             ],
             compiler_params=pltpu.CompilerParams(collective_id=0, has_side_effects=True),
         )(ctrl, pert, vertical_modes.T, mode_counts, slot_index, blend_weight)

time: 32.4 us -> 29.9 us (0.923)
  Pallas kernels: 32.2 us -> 29.6 us
    pallas_call x1, Pallas kernels: 31.3 us -> 28.7 us  [per_device(): pl.pallas_call(functools.partial(kernel, n_tm, n_mem, n_tile, members, wi...]
where the time goes in v4:
time: 29.9 us; the launch traced here: 29.6 us
  Pallas kernels  29.6 us (99%)
    pallas_call x1, Pallas kernels, per_device(): pl.pallas_call(functools.partial(kernel, n_tm, n_mem, n_tile, members, wi...  28.7 us
    pallas_call x1, Pallas kernels, per_device(): pl.pallas_call(blend_kernel, out_shape=jax.ShapeDtypeStruct((windows, lev...  0.94 us

profile of v4, /device:TPU:480, one launch (start us, length us, event | category | flops | bytes accessed | tf_op | source)
XLA Modules:
  0.0 29.6 jit_solution(2569618847827121064)
XLA Ops:
  0.0 28.7 %shard_map.64 = (f32[4,8,3,2,8,128]{5,4,3,2,1,0:T(8,128)S(1)}, f32[3,2,8,128]{3,2,1,0:T(8,128)S(1)}) custom-call(f32[160,128]{1,0:T(8,128)} %bitcast.17, bf16[10,2,32,16,128]{4,3,2,1,0:T(8,128)(2,1)} %bitcast.16, f32[2,64]{1,0:T(2,128)} %bitcast.18, s32[4]{0:T(128)} %counts_hbm.1, s32[3]{0:T(128)} %index_hbm.1, f32[3]{0:T(128)} %weight_hbm.1), custom_call_target="tpu_custom_call" | custom-call | tf_op jit(solution)/shard_map/pallas_call | solution.py:523
  28.7 0.9 %shard_map.65 = f32[3,64,8,128]{3,2,1,0:T(8,128)} custom-call(f32[4,8,3,2,8,128]{5,4,3,2,1,0:T(8,128)S(1)} %get-tuple-element.7.gath, f32[3,2,8,128]{3,2,1,0:T(8,128)S(1)} %get-tuple-element.8.scale), custom_call_target="tpu_custom_call" | custom-call | tf_op jit(solution)/shard_map/pallas_call | solution.py:544

commit v5 on v4

--- a/solution.py
+++ b/solution.py
@@ -17,48 +17,67 @@
 MESH = pl.DeviceIdType.MESH
 
 
-def smooth_group(halo, f_ref, counts, norm, group, rows):
+def spread():
+    a, b = 1.0 - 4.0 * DIFFUSION, DIFFUSION
+    weights = [[0.0] * (SMOOTH - d + 1) for d in range(SMOOTH + 1)]
+    for k in range(SMOOTH + 1):
+        for d in range(k % 2, k + 1, 2):
+            outer = math.comb(SMOOTH, k) * b**k * math.comb(k, (k - d) // 2)
+            for j in range(SMOOTH - k + 1):
+                weights[d][j] += outer * math.comb(SMOOTH - k, j) * a ** (SMOOTH - k - j) * b**j
+    return weights
+
+
+def add_rows(halo, total, group, rows, longitudes):
+    weights = spread()
     lane = lax.broadcasted_iota(jnp.int32, (rows, 128), 1)
     first, last = lane == 0, lane == 127
-    base = group * 64
-
-    def load(x, h):
+    for x in longitudes:
         tile, inner = (x + 4) // 4, x % 4
-        return halo[tile, pl.ds(base + h * 4 + inner, rows, 8), :]
-
-    field = {(x, h): load(x, h) for x in range(-4, 8) for h in range(2)}
-    for step in range(SMOOTH):
-        lo, hi = -3 + step, 7 - step
-        new = {}
-        for x in range(lo, hi):
-            pair = [field[x, 0], field[x, 1]]
-            up = [pltpu.roll(v, 1, 1) for v in pair]
-            down = [pltpu.roll(v, 127, 1) for v in pair]
-            lateral = [
-                jnp.where(first, 0.0, up[0]) + jnp.where(last, down[1], down[0]),
-                jnp.where(first, up[0], up[1]) + jnp.where(last, 0.0, down[1]),
-            ]
-            for h in range(2):
-                near = field[x - 1, h] + field[x + 1, h]
-                new[x, h] = (1.0 - 4.0 * DIFFUSION) * pair[h] + DIFFUSION * (
-                    near + lateral[h]
-                )
-        field = new
+        reach = [(r, abs(r - x)) for r in range(4) if abs(r - x) <= SMOOTH]
+        pair = [halo[tile, pl.ds(group * 64 + h * 4 + inner, rows, 8), :] for h in range(2)]
+        for j in range(SMOOTH - min(d for _, d in reach) + 1):
+            if j:
+                up = [pltpu.roll(v, 1, 1) for v in pair]
+                down = [pltpu.roll(v, 127, 1) for v in pair]
+                pair = [
+                    jnp.where(first, 0.0, up[0]) + jnp.where(last, down[1], down[0]),
+                    jnp.where(first, up[0], up[1]) + jnp.where(last, 0.0, down[1]),
+                ]
+            for r, d in reach:
+                if j <= SMOOTH - d:
+                    for h in range(2):
+                        term = weights[d][j] * pair[h]
+                        total[r, h] = total[r, h] + term if (r, h) in total else term
+
+
+def smooth_own(halo, own, group, rows):
+    total = {}
+    add_rows(halo, total, group, rows, range(4))
+    for (x, h), value in total.items():
+        own[group * 8 + h * 4 + x, pl.ds(0, rows)] = value
+
+
+def smooth_rest(halo, own, f_ref, counts, norm, group, rows):
+    total = {
+        (x, h): own[group * 8 + h * 4 + x, pl.ds(0, rows)] for x in range(4) for h in range(2)
+    }
+    add_rows(halo, total, group, rows, (-4, -3, -2, -1, 4, 5, 6, 7))
     mode = lax.broadcasted_iota(jnp.int32, (rows, 128), 0) % 2
     for x in range(4):
         scales = [jnp.where(m < counts[x], norm, 0.0) for m in range(2)]
         scale = jnp.where(mode == 0, scales[0], scales[1])
         for h in range(2):
-            f_ref[pl.ds(base + h * 4 + x, rows, 8), :] = field[x, h] * scale
+            f_ref[pl.ds(group * 64 + h * 4 + x, rows, 8), :] = total[x, h] * scale
 
 
 def kernel(
     n_tm, n_mem, n_tile, members, windows,
     ctrl, pert_hbm, modes_hbm, counts_hbm, index_hbm, weight_hbm,
     gath, scale,
-    halo, pert, f_ref, far, near, mail_far, mail,
+    halo, own, pert, f_ref, far, near, mail_far, mail,
     za_out, za_in, zb_in, zc_in, modes, counts, slot_index, weight,
-    load_sems, halo_sems, send, recv, ready_next, ready_back,
+    halo_sems, send, recv, ready_next, ready_back,
 ):
     t, m = lax.axis_index("tm"), lax.axis_index("mem")
     tile = lax.axis_index("tile")
@@ -100,7 +119,7 @@
         signal(barrier, back)
 
     loads = [
-        pltpu.make_async_copy(src, dst, load_sems.at[k])
+        pltpu.make_async_copy(src, dst, send.at[k])
         for k, (src, dst) in enumerate((
             (ctrl, halo.at[1]), (counts_hbm, counts), (modes_hbm, modes),
             (index_hbm, slot_index), (weight_hbm, weight), (pert_hbm, pert),
@@ -176,14 +195,18 @@
 
         lax.fori_loop(0, n_mem * nc, clear, 0)
 
+    fields = 2 * members
+    groups = [(k // 8, min(8, fields - k)) for k in range(0, fields, 8)]
+    with scope("own"):
+        for group, rows in groups:
+            smooth_own(halo, own, group, rows)
     with scope("halo"):
         to_right(next_tile).wait_recv()
         to_left(last_tile).wait_recv()
 
     with scope("smooth"):
-        fields = 2 * members
-        for group in range(0, fields, 8):
-            smooth_group(halo, f_ref, counts, norm, group // 8, min(8, fields - group))
+        for group, rows in groups:
+            smooth_rest(halo, own, f_ref, counts, norm, group, rows)
         loads[5].wait()
 
     def part(quarter, chunk, dst):
@@ -210,7 +233,7 @@
         else:
             lax.fori_loop(0, pairs, body, 0)
 
-    late = place >= run - 2
+    late = place >= run - 4
 
     half = nc // 2
     hops = nc * lc // HOP
@@ -235,8 +258,8 @@
         return [u for u in range(nc * lc // HOP) if c * lc < (u + 1) * HOP <= (c + 1) * lc]
 
     def chain(u):
-        own = pl.ds(u * HOP, HOP)
-        return channel(2, u, za_out.at[own], za_in.at[own], onward)
+        levels = pl.ds(u * HOP, HOP)
+        return channel(2, u, za_out.at[levels], za_in.at[levels], onward)
 
     def around(c):
         two = pl.ds((c - 1) * lc, 2 * lc)
@@ -316,11 +339,11 @@
                 around(c).start()
 
     def step_g(c):
-        own = both(gath.at[m, c])
+        mine = both(gath.at[m, c])
         for device in (right, left):
-            channel(4, c, own, own, device).start()
+            channel(4, c, mine, mine, device).start()
         if c >= half:
-            remote(own, own, send.at[5], recv.at[bases[4] + 1], across).start()
+            remote(mine, mine, send.at[5], recv.at[bases[4] + 1], across).start()
 
     def step_z2(c):
         for u in units(c):
@@ -407,8 +430,9 @@
     @pl.when(t == 1)
     def _():
         play([(step_b, c) for c in ringed] + [(step_g, c) for c in every])
+        play([(step_e, c, early_1) for c in range(half)])
         step_d()
-        play([(step_e, c, early_1) for c in every])
+        play([(step_e, c, early_1) for c in range(half, nc)])
 
     @pl.when((t == 2) & jnp.logical_not(late))
     def _():
@@ -529,7 +553,7 @@
             in_specs=[hbm] * 6,
             out_specs=(vmem, vmem),
             scratch_shapes=[
-                pltpu.VMEM((3, rows, 128), f32),
+                pltpu.VMEM((3, rows, 128), f32), pltpu.VMEM((8 * -(-2 * members // 8), 8, 128), f32),
                 pltpu.VMEM(pert.shape, jnp.bfloat16),
                 pltpu.VMEM((rows, 128), f32),
                 pltpu.VMEM(slot, f32), pltpu.VMEM((nc, 2, *slot[1:]), f32),
@@ -537,7 +561,7 @@
                 pltpu.VMEM(one, f32), pltpu.VMEM(one, f32), pltpu.VMEM(one, f32), pltpu.VMEM(one, f32),
                 pltpu.SMEM((2, levels), f32), pltpu.SMEM(mode_counts.shape, jnp.int32),
                 pltpu.SMEM((windows,), jnp.int32), pltpu.SMEM((windows,), f32),
-                dma((6,)), dma((5,)), dma((8,)), dma((2 * nc - DIRECT + nc * lc // HOP + nc + 4,)), regular, regular,
+                dma((5,)), dma((8,)), dma((2 * nc - DIRECT + nc * lc // HOP + nc + 4,)), regular, regular,
             ],
             compiler_params=pltpu.CompilerParams(collective_id=0, has_side_effects=True),
         )(ctrl, pert, vertical_modes.T, mode_counts, slot_index, blend_weight)

time: 29.9 us -> 29.6 us (0.990)
  Pallas kernels: 29.6 us -> 29.3 us
    pallas_call x1, Pallas kernels: 28.7 us -> 28.3 us  [per_device(): pl.pallas_call(functools.partial(kernel, n_tm, n_mem, n_tile, members, wi...]
where the time goes in v5:
time: 29.6 us; the launch traced here: 29.3 us
  Pallas kernels  29.3 us (99%)
    pallas_call x1, Pallas kernels, per_device(): pl.pallas_call(functools.partial(kernel, n_tm, n_mem, n_tile, members, wi...  28.3 us
    pallas_call x1, Pallas kernels, per_device(): pl.pallas_call(blend_kernel, out_shape=jax.ShapeDtypeStruct((windows, lev...  0.94 us

profile of v5, /device:TPU:480, one launch (start us, length us, event | category | flops | bytes accessed | tf_op | source)
XLA Modules:
  0.0 29.3 jit_solution(4924778752012406718)
XLA Ops:
  0.0 28.3 %shard_map.64 = (f32[4,8,3,2,8,128]{5,4,3,2,1,0:T(8,128)S(1)}, f32[3,2,8,128]{3,2,1,0:T(8,128)S(1)}) custom-call(f32[160,128]{1,0:T(8,128)} %bitcast.17, bf16[10,2,32,16,128]{4,3,2,1,0:T(8,128)(2,1)} %bitcast.16, f32[2,64]{1,0:T(2,128)} %bitcast.18, s32[4]{0:T(128)} %counts_hbm.1, s32[3]{0:T(128)} %index_hbm.1, f32[3]{0:T(128)} %weight_hbm.1), custom_call_target="tpu_custom_call" | custom-call | tf_op jit(solution)/shard_map/pallas_call | solution.py:547
  28.3 0.9 %shard_map.65 = f32[3,64,8,128]{3,2,1,0:T(8,128)} custom-call(f32[4,8,3,2,8,128]{5,4,3,2,1,0:T(8,128)S(1)} %get-tuple-element.7.gath, f32[3,2,8,128]{3,2,1,0:T(8,128)S(1)} %get-tuple-element.8.scale), custom_call_target="tpu_custom_call" | custom-call | tf_op jit(solution)/shard_map/pallas_call | solution.py:568

commit v6 on v5

--- a/solution.py
+++ b/solution.py
@@ -12,8 +12,8 @@
 SMOOTH = 4
 DIFFUSION = 0.24
 CHUNKS = 8
-HOP = 1
-DIRECT = 3
+HOP = 2
+DIRECT = 4
 MESH = pl.DeviceIdType.MESH
 
 

time: 29.6 us -> 29 us (0.980)
  the two profiles are of different devices: /device:TPU:480 before, /device:TPU:8 now
where the time goes in v6:
time: 29 us; the launch traced here: 28.9 us
  Pallas kernels  28.8 us (99%)
    pallas_call x1, Pallas kernels, per_device(): pl.pallas_call(functools.partial(kernel, n_tm, n_mem, n_tile, members, wi...  27.9 us
    pallas_call x1, Pallas kernels, per_device(): pl.pallas_call(blend_kernel, out_shape=jax.ShapeDtypeStruct((windows, lev...  0.94 us

profile of v6, /device:TPU:8, one launch (start us, length us, event | category | flops | bytes accessed | tf_op | source)
XLA Modules:
  0.0 28.9 jit_solution(15652609482463629590)
XLA Ops:
  0.0 27.9 %shard_map.64 = (f32[4,8,3,2,8,128]{5,4,3,2,1,0:T(8,128)S(1)}, f32[3,2,8,128]{3,2,1,0:T(8,128)S(1)}) custom-call(f32[160,128]{1,0:T(8,128)} %bitcast.17, bf16[10,2,32,16,128]{4,3,2,1,0:T(8,128)(2,1)} %bitcast.16, f32[2,64]{1,0:T(2,128)} %bitcast.18, s32[4]{0:T(128)} %counts_hbm.1, s32[3]{0:T(128)} %index_hbm.1, f32[3]{0:T(128)} %weight_hbm.1), custom_call_target="tpu_custom_call" | custom-call | tf_op jit(solution)/shard_map/pallas_call | solution.py:547
  27.9 0.9 %shard_map.65 = f32[3,64,8,128]{3,2,1,0:T(8,128)} custom-call(f32[4,8,3,2,8,128]{5,4,3,2,1,0:T(8,128)S(1)} %get-tuple-element.7.gath, f32[3,2,8,128]{3,2,1,0:T(8,128)S(1)} %get-tuple-element.8.scale), custom_call_target="tpu_custom_call" | custom-call | tf_op jit(solution)/shard_map/pallas_call | solution.py:568

commit v7 on v6

--- a/solution.py
+++ b/solution.py
@@ -403,10 +403,10 @@
     every = range(nc)
     first = [(step_a, c) for c in ringed[:1]]
     for k in range(max(DIRECT, nc - DIRECT - 1)):
+        if k < DIRECT:
+            first.append((step_b, k))
         if DIRECT + 1 + k < nc:
             first.append((step_a, DIRECT + 1 + k))
-        if k < DIRECT:
-            first.append((step_b, k))
     play(first)
 
     def rest(also=None):

time: 29 us -> 29.6 us (1.021)
  the two profiles are of different devices: /device:TPU:8 before, /device:TPU:480 now
where the time goes in v7:
time: 29.6 us; the launch traced here: 29.1 us
  Pallas kernels  29.1 us (98%)
    pallas_call x1, Pallas kernels, per_device(): pl.pallas_call(functools.partial(kernel, n_tm, n_mem, n_tile, members, wi...  28.1 us
    pallas_call x1, Pallas kernels, per_device(): pl.pallas_call(blend_kernel, out_shape=jax.ShapeDtypeStruct((windows, lev...  0.94 us

profile of v7, /device:TPU:480, one launch (start us, length us, event | category | flops | bytes accessed | tf_op | source)
XLA Modules:
  0.0 29.1 jit_solution(9449073875378868387)
XLA Ops:
  0.0 28.1 %shard_map.64 = (f32[4,8,3,2,8,128]{5,4,3,2,1,0:T(8,128)S(1)}, f32[3,2,8,128]{3,2,1,0:T(8,128)S(1)}) custom-call(f32[160,128]{1,0:T(8,128)} %bitcast.17, bf16[10,2,32,16,128]{4,3,2,1,0:T(8,128)(2,1)} %bitcast.16, f32[2,64]{1,0:T(2,128)} %bitcast.18, s32[4]{0:T(128)} %counts_hbm.1, s32[3]{0:T(128)} %index_hbm.1, f32[3]{0:T(128)} %weight_hbm.1), custom_call_target="tpu_custom_call" | custom-call | tf_op jit(solution)/shard_map/pallas_call | solution.py:547
  28.2 0.9 %shard_map.65 = f32[3,64,8,128]{3,2,1,0:T(8,128)} custom-call(f32[4,8,3,2,8,128]{5,4,3,2,1,0:T(8,128)S(1)} %get-tuple-element.7.gath, f32[3,2,8,128]{3,2,1,0:T(8,128)S(1)} %get-tuple-element.8.scale), custom_call_target="tpu_custom_call" | custom-call | tf_op jit(solution)/shard_map/pallas_call | solution.py:568
